TPU v7x, 128 devices: a whole 4x4x4 slice. The times are simulated.
128 devices in a mesh: lat: 8 (over z, core), lon: 16 (over y, x).
Axes of the slice: x: 4, y: 4, z: 4, core: 2. Of those that a mesh axis runs over, the one named last changes fastest.
Arguments:
- increments: bfloat16 [262144, 3, 128], P(('lat', 'lon')), may hold values from -6 to 6
- cotangent: bfloat16 [262144, 128], P(('lat', 'lon')), may hold values from -6 to 6
- owner_perm: int32 [128, 2048], P(('lat', 'lon')), may hold values from 0 to 2047, each once within a row
- coarse_index: int32 [2, 131072], P(None, ('lat', 'lon')), may hold values from 0 to 2047
- coarse_weight: float32 [131072], P(('lat', 'lon')), may hold values from 0.2 to 0.8
- back_index: int32 [2, 262144], P(None, ('lat', 'lon')), may hold values from 0 to 1023
- back_weight: float32 [262144], P(('lat', 'lon')), may hold values from 0.2 to 0.8
- lw_scale: float32 [16, 131072], P(None, ('lat', 'lon')), may hold values from 0.1 to 1
- sw_scale: float32 [14, 131072], P(None, ('lat', 'lon')), may hold values from 0.2 to 2
- sunlit: int32 [131072], P(('lat', 'lon')), may hold values from 0 to 1, as said below
- lw_table: bfloat16 [16, 3, 128, 128], P(None, None, 'lon'), may hold values from -0.3125 to 0.3125
- sw_table: bfloat16 [14, 3, 128, 128], P(None, None, 'lon'), may hold values from -0.3125 to 0.3125
Outputs:
- tendency: bfloat16 [262144, 128], P(('lat', 'lon'))
- gradient: bfloat16 [262144, 3, 128], P(('lat', 'lon'))
Inputs may be any that keep to these rules, and one draw needn't show every extreme that they name: In each device's block of 1024 radiation columns at most 640 are sunlit, and some device has exactly 640.
All inputs are finite; a program needn't handle non-finite values.
Results may differ from a plain program's by a relative error of at most 0.014.
Values may be sent and summed in bfloat16 or wider, within the bound.
No kernel may reach another device: no remote copies, remote signals or barrier semaphores. Data moves between devices by JAX's collectives and lax.ppermute only.
A program may use at most 64 MiB of HBM per device.

v0:
```python
import jax
import jax.numpy as jnp
from jax import lax
from jax.experimental import pallas as pl
from jax.experimental.pallas import tpu as pltpu
from jax.sharding import PartitionSpec as P


ALL = ("lat", "lon")
F32 = jnp.float32
BF16 = jnp.bfloat16
MIB = 1 << 20


def call(kernel, out, flops, limit, scratch=(), specs=None):
    extra = {} if specs is None else {"in_specs": specs}
    return pl.pallas_call(
        kernel,
        out_shape=out,
        **extra,
        scratch_shapes=scratch,
        compiler_params=pltpu.CompilerParams(vmem_limit_bytes=limit * MIB),
        cost_estimate=pl.CostEstimate(flops=flops, bytes_accessed=4 * MIB, transcendentals=0),
    )


def pick_kernel(perm_ref, planes_ref, last_ref, out_ref):
    total = perm_ref.shape[1]
    rows = 1024
    data = jnp.concatenate([planes_ref[v] for v in range(planes_ref.shape[0])] + [last_ref[...]], axis=1)

    def block(i, carry):
        start = pl.multiple_of(i * rows, rows)
        index = jnp.transpose(jnp.broadcast_to(perm_ref[:, pl.ds(start, rows)], (128, rows)))
        lanes = lax.broadcasted_iota(jnp.int32, (rows, total), 1)
        hot = (jnp.concatenate([index] * (total // 128), axis=1) == lanes).astype(F32).astype(BF16)
        out_ref[pl.ds(start, rows), :] = jnp.dot(hot, data, preferred_element_type=F32).astype(BF16)
        return carry

    lax.fori_loop(0, total // rows, block, 0)


def pick(perm, planes, last):
    total = perm.shape[1]
    width = (planes.shape[0] + 1) * 128
    out = jax.ShapeDtypeStruct((total, width), BF16)
    return call(pick_kernel, out, 2 * total * total * width, 20)(perm, planes, last)


def restore_kernel(perm_ref, data_ref, planes_ref, last_ref):
    total = perm_ref.shape[1]
    rows = 1024
    planes = planes_ref.shape[0]

    def block(i, carry):
        start = pl.multiple_of(i * rows, rows)
        targets = lax.broadcasted_iota(jnp.int32, (rows, total), 0) + start
        hot = (jnp.broadcast_to(perm_ref[...], (rows, total)) == targets).astype(F32).astype(BF16)
        got = jnp.dot(hot, data_ref[...], preferred_element_type=F32).astype(BF16)
        for v in range(planes):
            planes_ref[v, pl.ds(start, rows), :] = got[:, v * 128 : (v + 1) * 128]
        last_ref[pl.ds(start, rows), :] = got[:, planes * 128 :]
        return carry

    lax.fori_loop(0, total // rows, block, 0)


def restore(perm, data):
    total, width = data.shape
    planes = width // 128 - 1
    out = [
        jax.ShapeDtypeStruct((planes, total, 128), BF16),
        jax.ShapeDtypeStruct((total, 128), BF16),
    ]
    return call(restore_kernel, out, 2 * total * total * width, 20)(perm, data)


def two_hot(index_ref, share_ref, out_ref):
    rows, count = out_ref.shape
    block = 256
    first, second, share = index_ref[0:1, :], index_ref[1:2, :], share_ref[...]
    high = jnp.where(first == second, 1.0, share).astype(BF16)
    low = (1.0 - share).astype(BF16)
    targets = lax.broadcasted_iota(jnp.int32, (block, count), 0).astype(F32).astype(BF16)
    spread = lambda row: jnp.broadcast_to(row, (block, count))

    def step(i, carry):
        start = pl.multiple_of(i * block, block)
        one = spread((first - start).astype(F32).astype(BF16)) == targets
        two = spread((second - start).astype(F32).astype(BF16)) == targets
        out_ref[pl.ds(start, block), :] = jnp.where(
            one, spread(high), jnp.where(two, spread(low), jnp.zeros((), BF16))
        )
        return carry

    lax.fori_loop(0, rows // block, step, 0)


def radiation_kernel(
    data_ref,
    bidx_ref,
    bw_ref,
    cidx_ref,
    cw_ref,
    scale_ref,
    ta_hbm,
    tb_hbm,
    out_ref,
    ta_ref,
    tb_ref,
    sems,
    back_ref,
    coarse_ref,
    tt_ref,
    rows_ref,
    adj_ref,
    mid_ref,
    heat_ref,
):
    bands, width, _ = ta_ref.shape
    cols, _ = coarse_ref.shape
    half = 1024

    loads = [
        pltpu.make_async_copy(ta_hbm, ta_ref, sems.at[0]),
        pltpu.make_async_copy(tb_hbm, tb_ref, sems.at[1]),
    ]
    for load in loads:
        load.start()
    two_hot(bidx_ref, bw_ref, back_ref)
    two_hot(cidx_ref, cw_ref, coarse_ref)

    def adjoint(carry):
        adj_ref[...] = jnp.dot(back_ref[...], data_ref[:, width:], preferred_element_type=F32).T
        return carry

    def lift(carry):
        tables = [ref[b] for ref in (ta_ref, tb_ref) for b in range(bands)]
        lifted = jnp.concatenate(
            [(adj_ref[...] * scale_ref[b : b + 1, :]).astype(BF16) for b in range(2 * bands)], axis=0
        )
        got = jnp.dot(jnp.concatenate(tables, axis=1), lifted, preferred_element_type=F32)
        rows_ref[...] = got.T.astype(BF16)
        return carry

    def scatter(i, carry):
        start = pl.multiple_of(i * half, half)
        out_ref[pl.ds(start, half), :width] = jnp.dot(
            coarse_ref[pl.ds(start, half), :], rows_ref[...], preferred_element_type=F32
        ).astype(BF16)
        return carry

    def interpolate(carry):
        mid_ref[...] = lax.dot_general(
            data_ref[:, :width], coarse_ref[...], (((0,), (0,)), ((), ())), preferred_element_type=F32
        ).astype(BF16)
        return carry

    def heat(carry):
        lifted = jnp.concatenate(
            [
                mid_ref[...] * jnp.broadcast_to(scale_ref[b : b + 1, :].astype(BF16), mid_ref.shape)
                for b in range(2 * bands)
            ],
            axis=0,
        )
        heat_ref[...] = jnp.dot(tt_ref[...], lifted, preferred_element_type=F32).astype(BF16)
        return carry

    def back(carry):
        tendency = jnp.dot(heat_ref[...], back_ref[...], preferred_element_type=F32)
        out_ref[:, width:] = tendency.T.astype(BF16)
        return carry

    adjoint(0)
    for load in loads:
        load.wait()
    lift(0)
    lax.fori_loop(0, cols // half, scatter, 0)
    interpolate(0)
    for part, ref in enumerate((ta_ref, tb_ref)):
        for b in range(bands):
            at = (part * bands + b) * width
            tt_ref[:, at : at + width] = ref[b].T
    heat(0)
    back(0)


def radiation(data, bidx, bw, cidx, cw, scale, ta, tb):
    cols, rows = bw.shape[1], cw.shape[1]
    bands, width, levels = ta.shape
    out = jax.ShapeDtypeStruct((cols, width + levels), BF16)
    flops = 8 * bands * rows * levels * width
    scratch = [
        pltpu.VMEM(ta.shape, BF16),
        pltpu.VMEM(tb.shape, BF16),
        pltpu.SemaphoreType.DMA((2,)),
        pltpu.VMEM((rows, cols), BF16),
        pltpu.VMEM((cols, rows), BF16),
        pltpu.VMEM((levels, 2 * bands * width), BF16),
        pltpu.VMEM((rows, width), BF16),
        pltpu.VMEM((levels, rows), F32),
        pltpu.VMEM((width, rows), BF16),
        pltpu.VMEM((levels, rows), BF16),
    ]
    near, far = pl.BlockSpec(memory_space=pltpu.VMEM), pl.BlockSpec(memory_space=pl.ANY)
    specs = [near] * 6 + [far] * 2
    kernel = call(radiation_kernel, out, flops, 34, scratch, specs)
    return kernel(data, bidx, bw, cidx, cw, scale, ta, tb)


def gather_four(block, stride):
    lon = lax.axis_size("lon")
    place = lax.rem(lax.axis_index("lon") // stride, 4)
    size = block.shape[0]
    out = jnp.zeros((4 * size,) + block.shape[1:], block.dtype)
    got = [block]
    for shift in (1, 3, 2):
        pairs = []
        for a in range(lon):
            at = a // stride % 4
            pairs.append((a, a + ((at + shift) % 4 - at) * stride))
        got.append(lax.ppermute(block, "lon", pairs))
    for shift, piece in zip((0, 1, 3, 2), got):
        out = lax.dynamic_update_slice_in_dim(
            out, piece, lax.rem(place + 4 - shift, 4) * size, axis=0
        )
    return out


def exchange(values, axes):
    return lax.all_to_all(values, axes, split_axis=0, concat_axis=0, tiled=True)


def local(
    increments,
    cotangent,
    owner_perm,
    coarse_index,
    coarse_weight,
    back_index,
    back_weight,
    lw_scale,
    sw_scale,
    sunlit,
    lw_table,
    sw_table,
):
    lat = lax.axis_size("lat")
    core = lax.rem(lax.axis_index("lat"), 2)
    table = jnp.concatenate([lw_table, sw_table], axis=0)
    bands, _, _, levels = table.shape
    half = bands // 2
    mine = lax.dynamic_slice_in_dim(table, core * half, half, axis=0)
    column = gather_four(mine[None], 1)
    whole = gather_four(column, 4)
    partner = [(a, a + 1 - 2 * (a % 2)) for a in range(lat)]
    other = lax.ppermute(whole, "lat", partner)
    mine, other = (
        t.transpose(1, 2, 0, 3, 4).reshape(half, -1, levels) for t in (whole, other)
    )
    scale = jnp.concatenate([lw_scale, sw_scale * sunlit.astype(F32)[None, :]], axis=0)
    scale = jnp.where(core == 0, scale, jnp.roll(scale, half, axis=0))
    scale = jnp.pad(scale, ((0, 2), (0, 0)))

    cw = coarse_weight[None]
    bw = back_weight[None]
    planes = increments.transpose(1, 0, 2)
    data = pick(owner_perm, planes, cotangent)
    data = exchange(data, ALL)
    back = radiation(data, back_index, bw, coarse_index, cw, scale, mine, other)
    back = exchange(back, ALL)
    gradient, tendency = restore(owner_perm, back)
    return (tendency, gradient.transpose(1, 0, 2))


def solution(mesh):
    in_specs = (
        P(ALL, None, None),
        P(ALL, None),
        P(ALL, None),
        P(None, ALL),
        P(ALL),
        P(None, ALL),
        P(ALL),
        P(None, ALL),
        P(None, ALL),
        P(ALL),
        P(None, None, "lon", None),
        P(None, None, "lon", None),
    )
    out_specs = (P(ALL, None), P(ALL, None, None))
    return jax.shard_map(local, mesh=mesh, in_specs=in_specs, out_specs=out_specs, check_vma=False)
```

profile of v0, /device:TPU:1, one launch (start us, length us, event | category | flops | bytes accessed | tf_op | source)
XLA Modules:
  0.0 130.7 jit_solution(15476753974168902257)
XLA Ops:
  0.6 0.1 broadcast_in_dim.19
  0.7 1.0 constant_dynamic-update-slice_fusion.7
  1.7 2.1 %collective-permute-start = (bf16[1,15,3,8,128]{4,3,0,2,1:T(8,128)(2,1)S(1)}, bf16[1,15,3,8,128]{4,3,0,2,1:T(8,128)(2,1)S(1)}, u32[]{:S(2)}, u32[]{:S(2)}) collective-permute-start(bf16[1,15,3,8,128]{4,3,0,2,1:T(8,128)(2,1)S(1)} %get-tuple-element.7), channel_id=1, source_target_pairs={{0,1},{1,2},{2,3},{3,0},{4,5},{5,6},{6,7},{7,4},{8,9},{9,10},{10,1... | collective-permute-start | bytes 276488 | tf_op jit(solution)/shard_map/ppermute | solution.py:223
  3.8 1.3 %collective-permute-start.1 = (bf16[1,15,3,8,128]{4,3,0,2,1:T(8,128)(2,1)S(1)}, bf16[1,15,3,8,128]{4,3,0,2,1:T(8,128)(2,1)S(1)}, u32[]{:S(2)}, u32[]{:S(2)}) collective-permute-start(bf16[1,15,3,8,128]{4,3,0,2,1:T(8,128)(2,1)S(1)} %get-tuple-element.7), channel_id=1, source_target_pairs={{0,3},{1,0},{2,1},{3,2},{4,7},{5,4},{6,5},{7,6},{8,11},{9,8},{10,9... | collective-permute-start | bytes 276488 | tf_op jit(solution)/shard_map/ppermute | solution.py:223
  5.1 1.6 %collective-permute-start.2 = (bf16[1,15,3,8,128]{4,3,0,2,1:T(8,128)(2,1)S(1)}, bf16[1,15,3,8,128]{4,3,0,2,1:T(8,128)(2,1)S(1)}, u32[]{:S(2)}, u32[]{:S(2)}) collective-permute-start(bf16[1,15,3,8,128]{4,3,0,2,1:T(8,128)(2,1)S(1)} %get-tuple-element.7), channel_id=1, source_target_pairs={{0,2},{1,3},{2,0},{3,1},{4,6},{5,7},{6,4},{7,5},{8,10},{9,11},{10,... | collective-permute-start | bytes 276488 | tf_op jit(solution)/shard_map/ppermute | solution.py:223
  6.8 0.2 collective-permute-done
  7.0 0.2 collective-permute-done.1
  7.2 3.1 %collective-permute-done.2 = bf16[1,15,3,8,128]{4,3,0,2,1:T(8,128)(2,1)S(1)} collective-permute-done((bf16[1,15,3,8,128]{4,3,0,2,1:T(8,128)(2,1)S(1)}, bf16[1,15,3,8,128]{4,3,0,2,1:T(8,128)(2,1)S(1)}, u32[]{:S(2)}, u32[]{:S(2)}) %collective-permute-start.2) | collective-permute-done | bytes 92192 | tf_op jit(solution)/shard_map/ppermute | solution.py:223
  10.3 1.4 %collective-permute-start.3 = (bf16[4,15,3,8,128]{4,3,0,2,1:T(8,128)(2,1)S(1)}, bf16[4,15,3,8,128]{4,3,0,2,1:T(8,128)(2,1)}, u32[]{:S(2)}, u32[]{:S(2)}) collective-permute-start(bf16[4,15,3,8,128]{4,3,0,2,1:T(8,128)(2,1)S(1)} %constant_dynamic-update-slice_fusion.4), channel_id=1, source_target_pairs={{0,4},{1,5},{2,6},{3,7},{4,8},{5,9},{6,10},{7,11},{8,12},{9,13},{1... | collective-permute-start | bytes 1105928 | tf_op jit(solution)/shard_map/ppermute | solution.py:223
  11.7 1.5 %collective-permute-start.4 = (bf16[4,15,3,8,128]{4,3,0,2,1:T(8,128)(2,1)S(1)}, bf16[4,15,3,8,128]{4,3,0,2,1:T(8,128)(2,1)S(1)}, u32[]{:S(2)}, u32[]{:S(2)}) collective-permute-start(bf16[4,15,3,8,128]{4,3,0,2,1:T(8,128)(2,1)S(1)} %constant_dynamic-update-slice_fusion.4), channel_id=1, source_target_pairs={{0,12},{1,13},{2,14},{3,15},{4,0},{5,1},{6,2},{7,3},{8,4},{9,5},{1... | collective-permute-start | bytes 1105928 | tf_op jit(solution)/shard_map/ppermute | solution.py:223
  13.2 0.0 copy-start.1
  13.2 1.4 %copy-done.1 = bf16[2048,3,128]{2,0,1:T(8,128)(2,1)S(1)} copy-done((bf16[2048,3,128]{2,0,1:T(8,128)(2,1)S(1)}, bf16[2048,3,128]{2,0,1:T(8,128)(2,1)}, u32[]{:S(2)}) %copy-start.1) | copy-done | bytes 1572888
  14.6 1.0 copy-done.2
  15.7 0.0 copy-start.6
  15.7 0.7 copy-done.6
  16.4 4.9 %shard_map.131 = bf16[2048,512]{1,0:T(8,128)(2,1)S(1)} custom-call(s32[1,2048]{1,0:T(1,128)S(1)} %copy-done.6, bf16[3,2048,128]{2,1,0:T(8,128)(2,1)S(1)} %bitcast.21, bf16[2048,128]{1,0:T(8,128)(2,1)S(1)} %copy-done.2), custom_call_target="tpu_custom_call" | custom-call | flops 4294967296 | bytes 4194304 | tf_op jit(solution)/shard_map/pallas_call | solution.py:47
  21.2 0.0 copy-start
  21.3 1.3 %copy-done = bf16[2048,512]{1,0:T(8,128)(2,1)} copy-done((bf16[2048,512]{1,0:T(8,128)(2,1)}, bf16[2048,512]{1,0:T(8,128)(2,1)S(1)}, u32[]{:S(2)}) %copy-start) | copy-done | bytes 2097176
  22.6 10.2 %all-to-all-start = ((bf16[128,16,512]{2,1,0:T(8,128)(2,1)}), bf16[128,16,512]{2,1,0:T(8,128)(2,1)S(1)}, u32[]{:S(2)}, u32[]{:S(2)}) async-start(bf16[128,16,512]{2,1,0:T(8,128)(2,1)} %bitcast.18), calls=%async_computation | async-start | bytes 4194304 | tf_op jit(solution)/shard_map/all_to_all | solution.py:232
  32.8 2.9 %collective-permute-start.5 = (bf16[4,15,3,8,128]{4,3,0,2,1:T(8,128)(2,1)S(1)}, bf16[4,15,3,8,128]{4,3,0,2,1:T(8,128)(2,1)S(1)}, u32[]{:S(2)}, u32[]{:S(2)}) collective-permute-start(bf16[4,15,3,8,128]{4,3,0,2,1:T(8,128)(2,1)S(1)} %constant_dynamic-update-slice_fusion.4), channel_id=1, source_target_pairs={{0,8},{1,9},{2,10},{3,11},{4,12},{5,13},{6,14},{7,15},{8,0},{9,1},... | collective-permute-start | bytes 1105928 | tf_op jit(solution)/shard_map/ppermute | solution.py:223
  35.8 1.5 %broadcast_in_dim.18 = bf16[16,15,3,8,128]{4,3,0,2,1:T(8,128)(2,1)} broadcast(bf16[]{:T(256)} %constant.74.clone.1), dimensions={} | broadcast | bytes 1474562 | tf_op jit(solution)/shard_map/broadcast_in_dim | solution.py:216
  37.2 0.0 copy-start.11
  37.2 0.0 copy-start.10
  37.2 0.0 copy-start.9
  37.2 0.8 constant_dynamic-update-slice_fusion.3
  38.0 0.0 collective-permute-done.3
  38.0 1.8 %constant_dynamic-update-slice_fusion.2 = bf16[16,15,3,8,128]{4,3,0,2,1:T(8,128)(2,1)} fusion(bf16[16,15,3,8,128]{4,3,0,2,1:T(8,128)(2,1)} %constant_dynamic-update-slice_fusion.3, bf16[4,15,3,8,128]{4,3,0,2,1:T(8,128)(2,1)} %collective-permute-done.3, s32[]{:T(128)S(6)} %select_n.50), kind=kLoop, calls=%fused_computation.12 | loop fusion | bytes 737284 | tf_op jit(solution)/shard_map/dynamic_update_slice | solution.py:225
  39.8 0.0 copy-start.3
  39.8 0.0 copy-start.4
  39.8 0.0 collective-permute-done.4
  39.8 0.8 constant_dynamic-update-slice_fusion.1
  40.7 25.4 %collective-permute-done.5 = bf16[4,15,3,8,128]{4,3,0,2,1:T(8,128)(2,1)S(1)} collective-permute-done((bf16[4,15,3,8,128]{4,3,0,2,1:T(8,128)(2,1)S(1)}, bf16[4,15,3,8,128]{4,3,0,2,1:T(8,128)(2,1)S(1)}, u32[]{:S(2)}, u32[]{:S(2)}) %collective-permute-start.5) | collective-permute-done | bytes 368672 | tf_op jit(solution)/shard_map/ppermute | solution.py:223
  66.1 0.8 constant_dynamic-update-slice_fusion
  66.9 1.0 collective-permute-start.6
  67.8 0.0 copy-done.11
  67.8 0.0 copy-done.10
  67.8 0.0 copy-done.9
  67.9 3.1 %collective-permute-done.6 = bf16[16,15,3,8,128]{4,3,0,2,1:T(8,128)(2,1)} collective-permute-done((bf16[16,15,3,8,128]{4,3,0,2,1:T(8,128)(2,1)}, bf16[16,15,3,8,128]{4,3,0,2,1:T(8,128)(2,1)}, u32[]{:S(2)}, u32[]{:S(2)}) %collective-permute-start.6) | collective-permute-done | bytes 1474592 | tf_op jit(solution)/shard_map/ppermute | solution.py:258
  71.1 0.0 all-to-all-done
  71.1 0.0 copy-done.3
  71.1 0.0 copy-done.4
  71.1 0.0 copy-done.5
  71.1 0.0 copy-done.8
  71.1 16.4 %shard_map.132 = bf16[2048,512]{1,0:T(8,128)(2,1)S(1)} custom-call(bf16[2048,512]{1,0:T(8,128)(2,1)S(1)} %bitcast.17, s32[2,2048]{1,0:T(2,128)S(1)} %copy-done.3, f32[1,2048]{1,0:T(1,128)S(1)} %bitcast.22, s32[2,1024]{1,0:T(2,128)S(1)} %copy-done.5, f32[1,1024]{1,0:T(1,128)S(1)} %bitcast.23, f32[32,1024]{1,0:T(8,128)S(1)} %pad.4.scale_ref, ...), custom_call_target="tpu_custom_call" | custom-call | flops 6039797760 | bytes 4194304 | tf_op jit(solution)/shard_map/pallas_call | solution.py:209
  87.5 0.0 copy-start.7
  87.5 37.2 %all_to_all.22 = bf16[128,16,512]{2,1,0:T(8,128)(2,1)S(1)} all-to-all(bf16[128,16,512]{2,1,0:T(8,128)(2,1)S(1)} %bitcast.19), channel_id=1, replica_groups=mesh['lat'=8,'lon'=16] {'lat','lon'}, dimensions={0} | all-to-all | bytes 4194304 | tf_op jit(solution)/shard_map/all_to_all | solution.py:232
  124.7 0.0 copy-done.7
  124.7 6.0 %shard_map.133 = (bf16[3,2048,128]{2,1,0:T(8,128)(2,1)}, bf16[2048,128]{1,0:T(8,128)(2,1)}) custom-call(s32[1,2048]{1,0:T(1,128)S(1)} %copy-done.7, bf16[2048,512]{1,0:T(8,128)(2,1)S(1)} %bitcast.20), custom_call_target="tpu_custom_call" | custom-call | flops 4294967296 | bytes 4194304 | tf_op jit(solution)/shard_map/pallas_call | solution.py:75
  (11 shorter events, 0.1 us)
Async XLA Ops:
  1.7 5.3 %collective-permute-start = (bf16[1,15,3,8,128]{4,3,0,2,1:T(8,128)(2,1)S(1)}, bf16[1,15,3,8,128]{4,3,0,2,1:T(8,128)(2,1)S(1)}, u32[]{:S(2)}, u32[]{:S(2)}) collective-permute-start(bf16[1,15,3,8,128]{4,3,0,2,1:T(8,128)(2,1)S(1)} %get-tuple-element.7), channel_id=1, source_target_pairs={{0,1},{1,2},{2,3},{3,0},{4,5},{5,6},{6,7},{7,4},{8,9},{9,10},{10,1... | collective-permute-start | bytes 276488 | tf_op jit(solution)/shard_map/ppermute | solution.py:223
  3.8 3.4 %collective-permute-start.1 = (bf16[1,15,3,8,128]{4,3,0,2,1:T(8,128)(2,1)S(1)}, bf16[1,15,3,8,128]{4,3,0,2,1:T(8,128)(2,1)S(1)}, u32[]{:S(2)}, u32[]{:S(2)}) collective-permute-start(bf16[1,15,3,8,128]{4,3,0,2,1:T(8,128)(2,1)S(1)} %get-tuple-element.7), channel_id=1, source_target_pairs={{0,3},{1,0},{2,1},{3,2},{4,7},{5,4},{6,5},{7,6},{8,11},{9,8},{10,9... | collective-permute-start | bytes 276488 | tf_op jit(solution)/shard_map/ppermute | solution.py:223
  5.1 5.2 %collective-permute-start.2 = (bf16[1,15,3,8,128]{4,3,0,2,1:T(8,128)(2,1)S(1)}, bf16[1,15,3,8,128]{4,3,0,2,1:T(8,128)(2,1)S(1)}, u32[]{:S(2)}, u32[]{:S(2)}) collective-permute-start(bf16[1,15,3,8,128]{4,3,0,2,1:T(8,128)(2,1)S(1)} %get-tuple-element.7), channel_id=1, source_target_pairs={{0,2},{1,3},{2,0},{3,1},{4,6},{5,7},{6,4},{7,5},{8,10},{9,11},{10,... | collective-permute-start | bytes 276488 | tf_op jit(solution)/shard_map/ppermute | solution.py:223
  10.3 27.7 %collective-permute-start.3 = (bf16[4,15,3,8,128]{4,3,0,2,1:T(8,128)(2,1)S(1)}, bf16[4,15,3,8,128]{4,3,0,2,1:T(8,128)(2,1)}, u32[]{:S(2)}, u32[]{:S(2)}) collective-permute-start(bf16[4,15,3,8,128]{4,3,0,2,1:T(8,128)(2,1)S(1)} %constant_dynamic-update-slice_fusion.4), channel_id=1, source_target_pairs={{0,4},{1,5},{2,6},{3,7},{4,8},{5,9},{6,10},{7,11},{8,12},{9,13},{1... | collective-permute-start | bytes 1105928 | tf_op jit(solution)/shard_map/ppermute | solution.py:223
  11.7 28.1 %collective-permute-start.4 = (bf16[4,15,3,8,128]{4,3,0,2,1:T(8,128)(2,1)S(1)}, bf16[4,15,3,8,128]{4,3,0,2,1:T(8,128)(2,1)S(1)}, u32[]{:S(2)}, u32[]{:S(2)}) collective-permute-start(bf16[4,15,3,8,128]{4,3,0,2,1:T(8,128)(2,1)S(1)} %constant_dynamic-update-slice_fusion.4), channel_id=1, source_target_pairs={{0,12},{1,13},{2,14},{3,15},{4,0},{5,1},{6,2},{7,3},{8,4},{9,5},{1... | collective-permute-start | bytes 1105928 | tf_op jit(solution)/shard_map/ppermute | solution.py:223
  13.2 1.4 %copy-start.1 = (bf16[2048,3,128]{2,0,1:T(8,128)(2,1)S(1)}, bf16[2048,3,128]{2,0,1:T(8,128)(2,1)}, u32[]{:S(2)}) copy-start(bf16[2048,3,128]{2,0,1:T(8,128)(2,1)} %param.12) | copy-start | bytes 4718596
  14.6 1.0 copy-start.2
  15.7 0.7 copy-start.6
  21.2 1.3 %copy-start = (bf16[2048,512]{1,0:T(8,128)(2,1)}, bf16[2048,512]{1,0:T(8,128)(2,1)S(1)}, u32[]{:S(2)}) copy-start(bf16[2048,512]{1,0:T(8,128)(2,1)S(1)} %shard_map.131) | copy-start | bytes 6291460
  22.6 48.5 %all-to-all-start = ((bf16[128,16,512]{2,1,0:T(8,128)(2,1)}), bf16[128,16,512]{2,1,0:T(8,128)(2,1)S(1)}, u32[]{:S(2)}, u32[]{:S(2)}) async-start(bf16[128,16,512]{2,1,0:T(8,128)(2,1)} %bitcast.18), calls=%async_computation | async-start | bytes 4194304 | tf_op jit(solution)/shard_map/all_to_all | solution.py:232
  32.8 33.2 %collective-permute-start.5 = (bf16[4,15,3,8,128]{4,3,0,2,1:T(8,128)(2,1)S(1)}, bf16[4,15,3,8,128]{4,3,0,2,1:T(8,128)(2,1)S(1)}, u32[]{:S(2)}, u32[]{:S(2)}) collective-permute-start(bf16[4,15,3,8,128]{4,3,0,2,1:T(8,128)(2,1)S(1)} %constant_dynamic-update-slice_fusion.4), channel_id=1, source_target_pairs={{0,8},{1,9},{2,10},{3,11},{4,12},{5,13},{6,14},{7,15},{8,0},{9,1},... | collective-permute-start | bytes 1105928 | tf_op jit(solution)/shard_map/ppermute | solution.py:223
  37.2 30.6 %copy-start.11 = (s32[1024]{0:T(1024)S(1)}, s32[1024]{0:T(1024)}, u32[]{:S(2)}) copy-start(s32[1024]{0:T(1024)} %param.21) | copy-start | bytes 12292
  37.2 30.6 %copy-start.10 = (f32[14,1024]{1,0:T(8,128)S(1)}, f32[14,1024]{1,0:T(8,128)}, u32[]{:S(2)}) copy-start(f32[14,1024]{1,0:T(8,128)} %param.20) | copy-start | bytes 172036
  37.2 30.6 %copy-start.9 = (f32[16,1024]{1,0:T(8,128)S(1)}, f32[16,1024]{1,0:T(8,128)}, u32[]{:S(2)}) copy-start(f32[16,1024]{1,0:T(8,128)} %param.19) | copy-start | bytes 196612
  39.8 31.3 %copy-start.3 = (s32[2,2048]{1,0:T(2,128)S(1)}, s32[2,2048]{1,0:T(2,128)}, u32[]{:S(2)}) copy-start(s32[2,2048]{1,0:T(2,128)} %bidx_ref.1) | copy-start | bytes 49156
  39.8 31.3 %copy-start.4 = (f32[2048]{0:T(1024)S(1)}, f32[2048]{0:T(1024)}, u32[]{:S(2)}) copy-start(f32[2048]{0:T(1024)} %param.18) | copy-start | bytes 24580
  39.8 31.3 %copy-start.5 = (s32[2,1024]{1,0:T(2,128)S(1)}, s32[2,1024]{1,0:T(2,128)}, u32[]{:S(2)}) copy-start(s32[2,1024]{1,0:T(2,128)} %cidx_ref.1) | copy-start | bytes 24580
  39.8 31.3 %copy-start.8 = (f32[1024]{0:T(1024)S(1)}, f32[1024]{0:T(1024)}, u32[]{:S(2)}) copy-start(f32[1024]{0:T(1024)} %param.16) | copy-start | bytes 12292
  66.9 4.2 %collective-permute-start.6 = (bf16[16,15,3,8,128]{4,3,0,2,1:T(8,128)(2,1)}, bf16[16,15,3,8,128]{4,3,0,2,1:T(8,128)(2,1)}, u32[]{:S(2)}, u32[]{:S(2)}) collective-permute-start(bf16[16,15,3,8,128]{4,3,0,2,1:T(8,128)(2,1)} %constant_dynamic-update-slice_fusion), channel_id=1, source_target_pairs={{0,16},{16,0},{32,48},{48,32},{64,80},{80,64},{96,112},{112,96},{1... | collective-permute-start | bytes 4423688 | tf_op jit(solution)/shard_map/ppermute | solution.py:258
  87.5 37.2 %copy-start.7 = (s32[1,2048]{1,0:T(1,128)S(1)}, s32[1,2048]{1,0:T(1,128)}, u32[]{:S(2)}) copy-start(s32[1,2048]{1,0:T(1,128)} %perm_ref.3) | copy-start | bytes 24580
where the time goes:
time: 131 us
  blocking collectives  37.2 us (28%)
  waiting for transfers between devices  32 us (24%)
  Pallas kernels  27.2 us (21%)
  starting transfers between devices  22.1 us (17%)
  local copies, waits for them, and re-layouts  10.3 us (8%)
    all_to_all x1, blocking collectives, exchange(): return lax.all_to_all(values, axes, split_axis=0, concat_axis=0, tiled=True)  37.2 us
    ppermute x6, waiting for transfers between devices, gather_four(): got.append(lax.ppermute(block, 'lon', pairs))  28.9 us
    pallas_call x1, Pallas kernels, radiation(): return kernel(data, bidx, bw, cidx, cw, scale, ta, tb)  16.4 us
    ppermute x6, starting transfers between devices, gather_four(): got.append(lax.ppermute(block, 'lon', pairs))  10.9 us
    all_to_all x1, starting transfers between devices, exchange(): return lax.all_to_all(values, axes, split_axis=0, concat_axis=0, tiled=True)  10.2 us
    pallas_call x1, Pallas kernels, restore(): return call(restore_kernel, out, 2 * total * total * width, 20)(perm, data)  5.96 us
    pallas_call x1, Pallas kernels, pick(): call(pick_kernel, out, 2 * total * total * width, 20)(perm, planes, last)  4.88 us
    unnamed x24, local copies, waits for them, and re-layouts  4.49 us
  transfers between devices with their start and end apart: 8, of which 5 were waited for; matrix products, arithmetic and copies ran while one was open for 4% of the time, Pallas kernels for 4%

commit v1 on v0

--- a/solution.py
+++ b/solution.py
@@ -12,8 +12,10 @@
 MIB = 1 << 20
 
 
-def call(kernel, out, flops, limit, scratch=(), specs=None):
+def call(kernel, out, flops, limit, scratch=(), specs=None, out_specs=None):
     extra = {} if specs is None else {"in_specs": specs}
+    if out_specs is not None:
+        extra["out_specs"] = out_specs
     return pl.pallas_call(
         kernel,
         out_shape=out,
@@ -24,45 +26,100 @@
     )
 
 
-def pick_kernel(perm_ref, planes_ref, last_ref, out_ref):
+PICK_BLOCKS = (512, 512, 512, 512)
+
+
+def starts(blocks):
+    return [sum(blocks[:k]) for k in range(len(blocks))]
+
+
+def pick_kernel(perm_hbm, planes_hbm, last_hbm, out_hbm, perm_ref, data_ref, hot_ref, out_ref, in_sems, out_sems):
     total = perm_ref.shape[1]
-    rows = 1024
-    data = jnp.concatenate([planes_ref[v] for v in range(planes_ref.shape[0])] + [last_ref[...]], axis=1)
-
-    def block(i, carry):
-        start = pl.multiple_of(i * rows, rows)
-        index = jnp.transpose(jnp.broadcast_to(perm_ref[:, pl.ds(start, rows)], (128, rows)))
+    planes = planes_hbm.shape[0]
+    first = pltpu.make_async_copy(perm_hbm, perm_ref, in_sems.at[planes + 1])
+    first.start()
+    loads = [pltpu.make_async_copy(planes_hbm.at[v], data_ref.at[v], in_sems.at[v]) for v in range(planes)]
+    loads.append(pltpu.make_async_copy(last_hbm, data_ref.at[planes], in_sems.at[planes]))
+    for load in loads:
+        load.start()
+    first.wait()
+
+    def fill(k):
+        start, rows = starts(PICK_BLOCKS)[k], PICK_BLOCKS[k]
+        index = jnp.transpose(jnp.broadcast_to(perm_ref[:, start : start + rows], (128, rows)))
         lanes = lax.broadcasted_iota(jnp.int32, (rows, total), 1)
-        hot = (jnp.concatenate([index] * (total // 128), axis=1) == lanes).astype(F32).astype(BF16)
-        out_ref[pl.ds(start, rows), :] = jnp.dot(hot, data, preferred_element_type=F32).astype(BF16)
-        return carry
-
-    lax.fori_loop(0, total // rows, block, 0)
+        hot = jnp.concatenate([index] * (total // 128), axis=1) == lanes
+        hot_ref[k % 2, :rows, :] = hot.astype(F32).astype(BF16)
+
+    fill(0)
+    for load in loads:
+        load.wait()
+    stores = []
+    for k, (start, rows) in enumerate(zip(starts(PICK_BLOCKS), PICK_BLOCKS)):
+        data = jnp.concatenate([data_ref[v] for v in range(planes + 1)], axis=1)
+        got = jnp.dot(hot_ref[k % 2, :rows, :], data, preferred_element_type=F32)
+        out_ref[start : start + rows, :] = got.astype(BF16)
+        stores.append(
+            pltpu.make_async_copy(
+                out_ref.at[pl.ds(start, rows), :], out_hbm.at[pl.ds(start, rows), :], out_sems.at[k]
+            )
+        )
+        stores[-1].start()
+        if k + 1 < len(PICK_BLOCKS):
+            fill(k + 1)
+    for store in stores:
+        store.wait()
 
 
 def pick(perm, planes, last):
     total = perm.shape[1]
-    width = (planes.shape[0] + 1) * 128
-    out = jax.ShapeDtypeStruct((total, width), BF16)
-    return call(pick_kernel, out, 2 * total * total * width, 20)(perm, planes, last)
-
-
-def restore_kernel(perm_ref, data_ref, planes_ref, last_ref):
+    count = planes.shape[0] + 1
+    out = jax.ShapeDtypeStruct((total, count * 128), BF16)
+    far = pl.BlockSpec(memory_space=pl.ANY)
+    scratch = [
+        pltpu.VMEM(perm.shape, jnp.int32),
+        pltpu.VMEM((count, total, 128), BF16),
+        pltpu.VMEM((2, max(PICK_BLOCKS), total), BF16),
+        pltpu.VMEM((total, count * 128), BF16),
+        pltpu.SemaphoreType.DMA((count + 1,)),
+        pltpu.SemaphoreType.DMA((len(PICK_BLOCKS),)),
+    ]
+    flops = 2 * total * total * count * 128
+    return call(pick_kernel, out, flops, 60, scratch, [far] * 3, far)(perm, planes, last)
+
+
+RESTORE_BLOCKS = (1024, 512, 512)
+
+
+def restore_kernel(perm_ref, data_ref, planes_hbm, last_hbm, hot_ref, out_ref, sems):
     total = perm_ref.shape[1]
-    rows = 1024
-    planes = planes_ref.shape[0]
-
-    def block(i, carry):
-        start = pl.multiple_of(i * rows, rows)
+    planes = planes_hbm.shape[0]
+
+    def fill(k):
+        start, rows = starts(RESTORE_BLOCKS)[k], RESTORE_BLOCKS[k]
         targets = lax.broadcasted_iota(jnp.int32, (rows, total), 0) + start
-        hot = (jnp.broadcast_to(perm_ref[...], (rows, total)) == targets).astype(F32).astype(BF16)
-        got = jnp.dot(hot, data_ref[...], preferred_element_type=F32).astype(BF16)
-        for v in range(planes):
-            planes_ref[v, pl.ds(start, rows), :] = got[:, v * 128 : (v + 1) * 128]
-        last_ref[pl.ds(start, rows), :] = got[:, planes * 128 :]
-        return carry
-
-    lax.fori_loop(0, total // rows, block, 0)
+        hot = jnp.broadcast_to(perm_ref[...], (rows, total)) == targets
+        hot_ref[k % 2, :rows, :] = hot.astype(F32).astype(BF16)
+
+    fill(0)
+    stores = []
+    for k, (start, rows) in enumerate(zip(starts(RESTORE_BLOCKS), RESTORE_BLOCKS)):
+        got = jnp.dot(hot_ref[k % 2, :rows, :], data_ref[...], preferred_element_type=F32).astype(BF16)
+        for v in range(planes + 1):
+            out_ref[v, start : start + rows, :] = got[:, v * 128 : (v + 1) * 128]
+        span = pl.ds(start, rows)
+        stores.append(
+            pltpu.make_async_copy(
+                out_ref.at[pl.ds(0, planes), span, :], planes_hbm.at[:, span, :], sems.at[k, 0]
+            )
+        )
+        stores.append(pltpu.make_async_copy(out_ref.at[planes, span, :], last_hbm.at[span, :], sems.at[k, 1]))
+        stores[-2].start()
+        stores[-1].start()
+        if k + 1 < len(RESTORE_BLOCKS):
+            fill(k + 1)
+    for store in stores:
+        store.wait()
 
 
 def restore(perm, data):
@@ -72,7 +129,14 @@
         jax.ShapeDtypeStruct((planes, total, 128), BF16),
         jax.ShapeDtypeStruct((total, 128), BF16),
     ]
-    return call(restore_kernel, out, 2 * total * total * width, 20)(perm, data)
+    near, far = pl.BlockSpec(memory_space=pltpu.VMEM), pl.BlockSpec(memory_space=pl.ANY)
+    scratch = [
+        pltpu.VMEM((2, max(RESTORE_BLOCKS), total), BF16),
+        pltpu.VMEM((planes + 1, total, 128), BF16),
+        pltpu.SemaphoreType.DMA((len(RESTORE_BLOCKS), 2)),
+    ]
+    flops = 2 * total * total * width
+    return call(restore_kernel, out, flops, 40, scratch, [near] * 2, [far] * 2)(perm, data)
 
 
 def two_hot(index_ref, share_ref, out_ref):
@@ -118,8 +182,7 @@
     heat_ref,
 ):
     bands, width, _ = ta_ref.shape
-    cols, _ = coarse_ref.shape
-    half = 1024
+    cols, rows = coarse_ref.shape
 
     loads = [
         pltpu.make_async_copy(ta_hbm, ta_ref, sems.at[0]),
@@ -130,60 +193,67 @@
     two_hot(bidx_ref, bw_ref, back_ref)
     two_hot(cidx_ref, cw_ref, coarse_ref)
 
-    def adjoint(carry):
-        adj_ref[...] = jnp.dot(back_ref[...], data_ref[:, width:], preferred_element_type=F32).T
-        return carry
-
-    def lift(carry):
+    def adjoint(i, carry):
+        s = pl.multiple_of(i * 512, 512)
+        adj_ref[:, pl.ds(s, 512)] = jnp.dot(back_ref[pl.ds(s, 512), :], data_ref[:, width:], preferred_element_type=F32).T
+        return carry
+
+    def lift(i, carry):
+        s = pl.multiple_of(i * 1024, 1024)
         tables = [ref[b] for ref in (ta_ref, tb_ref) for b in range(bands)]
+        adj = adj_ref[:, pl.ds(s, 1024)]
         lifted = jnp.concatenate(
-            [(adj_ref[...] * scale_ref[b : b + 1, :]).astype(BF16) for b in range(2 * bands)], axis=0
+            [(adj * scale_ref[b : b + 1, pl.ds(s, 1024)]).astype(BF16) for b in range(2 * bands)], axis=0
         )
         got = jnp.dot(jnp.concatenate(tables, axis=1), lifted, preferred_element_type=F32)
-        rows_ref[...] = got.T.astype(BF16)
+        rows_ref[pl.ds(s, 1024), :] = got.T.astype(BF16)
         return carry
 
     def scatter(i, carry):
-        start = pl.multiple_of(i * half, half)
-        out_ref[pl.ds(start, half), :width] = jnp.dot(
-            coarse_ref[pl.ds(start, half), :], rows_ref[...], preferred_element_type=F32
+        start = pl.multiple_of(i * 1024, 1024)
+        out_ref[pl.ds(start, 1024), :width] = jnp.dot(
+            coarse_ref[pl.ds(start, 1024), :], rows_ref[...], preferred_element_type=F32
         ).astype(BF16)
         return carry
 
-    def interpolate(carry):
-        mid_ref[...] = lax.dot_general(
-            data_ref[:, :width], coarse_ref[...], (((0,), (0,)), ((), ())), preferred_element_type=F32
+    def interpolate(i, carry):
+        s = pl.multiple_of(i * 1024, 1024)
+        mid_ref[:, pl.ds(s, 1024)] = lax.dot_general(
+            data_ref[:, :width], coarse_ref[:, pl.ds(s, 1024)], (((0,), (0,)), ((), ())), preferred_element_type=F32
         ).astype(BF16)
         return carry
 
-    def heat(carry):
+    def heat(i, carry):
+        s = pl.multiple_of(i * 1024, 1024)
+        mid = mid_ref[:, pl.ds(s, 1024)]
         lifted = jnp.concatenate(
             [
-                mid_ref[...] * jnp.broadcast_to(scale_ref[b : b + 1, :].astype(BF16), mid_ref.shape)
+                mid * jnp.broadcast_to(scale_ref[b : b + 1, pl.ds(s, 1024)].astype(BF16), mid.shape)
                 for b in range(2 * bands)
             ],
             axis=0,
         )
-        heat_ref[...] = jnp.dot(tt_ref[...], lifted, preferred_element_type=F32).astype(BF16)
-        return carry
-
-    def back(carry):
-        tendency = jnp.dot(heat_ref[...], back_ref[...], preferred_element_type=F32)
-        out_ref[:, width:] = tendency.T.astype(BF16)
-        return carry
-
-    adjoint(0)
+        heat_ref[:, pl.ds(s, 1024)] = jnp.dot(tt_ref[...], lifted, preferred_element_type=F32).astype(BF16)
+        return carry
+
+    def back(i, carry):
+        s = pl.multiple_of(i * 2048, 2048)
+        tendency = jnp.dot(heat_ref[...], back_ref[:, pl.ds(s, 2048)], preferred_element_type=F32)
+        out_ref[pl.ds(s, 2048), width:] = tendency.T.astype(BF16)
+        return carry
+
+    lax.fori_loop(0, rows // 512, adjoint, 0)
     for load in loads:
         load.wait()
-    lift(0)
-    lax.fori_loop(0, cols // half, scatter, 0)
-    interpolate(0)
+    lax.fori_loop(0, rows // 1024, lift, 0)
+    lax.fori_loop(0, cols // 1024, scatter, 0)
+    lax.fori_loop(0, rows // 1024, interpolate, 0)
     for part, ref in enumerate((ta_ref, tb_ref)):
         for b in range(bands):
             at = (part * bands + b) * width
             tt_ref[:, at : at + width] = ref[b].T
-    heat(0)
-    back(0)
+    lax.fori_loop(0, rows // 1024, heat, 0)
+    lax.fori_loop(0, cols // 2048, back, 0)
 
 
 def radiation(data, bidx, bw, cidx, cw, scale, ta, tb):

time: 131 us -> 126 us (0.962)
  local copies, waits for them, and re-layouts: 10.3 us -> 5.83 us
    unnamed x24 -> x16, local copies, waits for them, and re-layouts: 4.49 us -> 0.03 us
    pallas_call x1, Pallas kernels: 16.4 us -> 14.5 us  [radiation(): return kernel(data, bidx, bw, cidx, cw, scale, ta, tb)]
    pallas_call x2, Pallas kernels: 10.8 us -> 12.3 us  [the longest x1 6.93 us: pick(): call(pick_kernel, out, flops, 60, scratch, [far] * 3, far)]
  transfers between devices with their start and end apart: 8 -> 8, of which waited for: 5 -> 5; matrix products, arithmetic and copies ran while one was open for 4% -> 5% of each run, Pallas kernels for 4% -> 6%
where the time goes in v1:
time: 126 us
  blocking collectives  37.2 us (30%)
  waiting for transfers between devices  32 us (25%)
  Pallas kernels  26.8 us (21%)
  starting transfers between devices  22.1 us (18%)
  local copies, waits for them, and re-layouts  5.83 us (5%)
    all_to_all x1, blocking collectives, exchange(): return lax.all_to_all(values, axes, split_axis=0, concat_axis=0, tiled=True)  37.2 us
    ppermute x6, waiting for transfers between devices, gather_four(): got.append(lax.ppermute(block, 'lon', pairs))  28.9 us
    pallas_call x1, Pallas kernels, radiation(): return kernel(data, bidx, bw, cidx, cw, scale, ta, tb)  14.5 us
    ppermute x6, starting transfers between devices, gather_four(): got.append(lax.ppermute(block, 'lon', pairs))  10.9 us
    all_to_all x1, starting transfers between devices, exchange(): return lax.all_to_all(values, axes, split_axis=0, concat_axis=0, tiled=True)  10.2 us
    pallas_call x1, Pallas kernels, pick(): call(pick_kernel, out, flops, 60, scratch, [far] * 3, far)  6.93 us
    pallas_call x1, Pallas kernels, restore(): call(restore_kernel, out, flops, 40, scratch, [near] * 2, [far] * 2)  5.33 us
    dynamic_update_slice x7, local copies, waits for them, and re-layouts, gather_four(): lax.dynamic_update_slice_in_dim(out, piece, lax.rem(place + 4 - shift, 4)...  4.28 us
  transfers between devices with their start and end apart: 8, of which 5 were waited for; matrix products, arithmetic and copies ran while one was open for 5% of the time, Pallas kernels for 6%

profile of v1, /device:TPU:1, one launch (start us, length us, event | category | flops | bytes accessed | tf_op | source)
XLA Modules:
  0.0 125.9 jit_solution(11993366632941936698)
XLA Ops:
  0.6 0.1 broadcast_in_dim.19
  0.7 1.0 constant_dynamic-update-slice_fusion.7
  1.7 2.1 %collective-permute-start = (bf16[1,15,3,8,128]{4,3,0,2,1:T(8,128)(2,1)S(1)}, bf16[1,15,3,8,128]{4,3,0,2,1:T(8,128)(2,1)S(1)}, u32[]{:S(2)}, u32[]{:S(2)}) collective-permute-start(bf16[1,15,3,8,128]{4,3,0,2,1:T(8,128)(2,1)S(1)} %get-tuple-element.7), channel_id=1, source_target_pairs={{0,1},{1,2},{2,3},{3,0},{4,5},{5,6},{6,7},{7,4},{8,9},{9,10},{10,1... | collective-permute-start | bytes 276488 | tf_op jit(solution)/shard_map/ppermute | solution.py:293
  3.8 1.3 %collective-permute-start.1 = (bf16[1,15,3,8,128]{4,3,0,2,1:T(8,128)(2,1)S(1)}, bf16[1,15,3,8,128]{4,3,0,2,1:T(8,128)(2,1)S(1)}, u32[]{:S(2)}, u32[]{:S(2)}) collective-permute-start(bf16[1,15,3,8,128]{4,3,0,2,1:T(8,128)(2,1)S(1)} %get-tuple-element.7), channel_id=1, source_target_pairs={{0,3},{1,0},{2,1},{3,2},{4,7},{5,4},{6,5},{7,6},{8,11},{9,8},{10,9... | collective-permute-start | bytes 276488 | tf_op jit(solution)/shard_map/ppermute | solution.py:293
  5.1 1.6 %collective-permute-start.2 = (bf16[1,15,3,8,128]{4,3,0,2,1:T(8,128)(2,1)S(1)}, bf16[1,15,3,8,128]{4,3,0,2,1:T(8,128)(2,1)S(1)}, u32[]{:S(2)}, u32[]{:S(2)}) collective-permute-start(bf16[1,15,3,8,128]{4,3,0,2,1:T(8,128)(2,1)S(1)} %get-tuple-element.7), channel_id=1, source_target_pairs={{0,2},{1,3},{2,0},{3,1},{4,6},{5,7},{6,4},{7,5},{8,10},{9,11},{10,... | collective-permute-start | bytes 276488 | tf_op jit(solution)/shard_map/ppermute | solution.py:293
  6.8 0.2 collective-permute-done
  7.0 0.2 collective-permute-done.1
  7.2 3.1 %collective-permute-done.2 = bf16[1,15,3,8,128]{4,3,0,2,1:T(8,128)(2,1)S(1)} collective-permute-done((bf16[1,15,3,8,128]{4,3,0,2,1:T(8,128)(2,1)S(1)}, bf16[1,15,3,8,128]{4,3,0,2,1:T(8,128)(2,1)S(1)}, u32[]{:S(2)}, u32[]{:S(2)}) %collective-permute-start.2) | collective-permute-done | bytes 92192 | tf_op jit(solution)/shard_map/ppermute | solution.py:293
  10.3 1.4 %collective-permute-start.3 = (bf16[4,15,3,8,128]{4,3,0,2,1:T(8,128)(2,1)S(1)}, bf16[4,15,3,8,128]{4,3,0,2,1:T(8,128)(2,1)}, u32[]{:S(2)}, u32[]{:S(2)}) collective-permute-start(bf16[4,15,3,8,128]{4,3,0,2,1:T(8,128)(2,1)S(1)} %constant_dynamic-update-slice_fusion.4), channel_id=1, source_target_pairs={{0,4},{1,5},{2,6},{3,7},{4,8},{5,9},{6,10},{7,11},{8,12},{9,13},{1... | collective-permute-start | bytes 1105928 | tf_op jit(solution)/shard_map/ppermute | solution.py:293
  11.7 1.5 %collective-permute-start.4 = (bf16[4,15,3,8,128]{4,3,0,2,1:T(8,128)(2,1)S(1)}, bf16[4,15,3,8,128]{4,3,0,2,1:T(8,128)(2,1)S(1)}, u32[]{:S(2)}, u32[]{:S(2)}) collective-permute-start(bf16[4,15,3,8,128]{4,3,0,2,1:T(8,128)(2,1)S(1)} %constant_dynamic-update-slice_fusion.4), channel_id=1, source_target_pairs={{0,12},{1,13},{2,14},{3,15},{4,0},{5,1},{6,2},{7,3},{8,4},{9,5},{1... | collective-permute-start | bytes 1105928 | tf_op jit(solution)/shard_map/ppermute | solution.py:293
  13.2 6.9 %shard_map.131 = bf16[2048,512]{1,0:T(8,128)(2,1)} custom-call(s32[1,2048]{1,0:T(1,128)} %perm_ref.1, bf16[3,2048,128]{2,1,0:T(8,128)(2,1)} %bitcast.23, bf16[2048,128]{1,0:T(8,128)(2,1)} %last_hbm.1), custom_call_target="tpu_custom_call" | custom-call | flops 4294967296 | bytes 4194304 | tf_op jit(solution)/shard_map/pallas_call | solution.py:88
  20.1 10.2 %all-to-all-start = ((bf16[128,16,512]{2,1,0:T(8,128)(2,1)}), bf16[128,16,512]{2,1,0:T(8,128)(2,1)S(1)}, u32[]{:S(2)}, u32[]{:S(2)}) async-start(bf16[128,16,512]{2,1,0:T(8,128)(2,1)} %bitcast.22), calls=%async_computation | async-start | bytes 4194304 | tf_op jit(solution)/shard_map/all_to_all | solution.py:302
  30.4 2.9 %collective-permute-start.5 = (bf16[4,15,3,8,128]{4,3,0,2,1:T(8,128)(2,1)S(1)}, bf16[4,15,3,8,128]{4,3,0,2,1:T(8,128)(2,1)S(1)}, u32[]{:S(2)}, u32[]{:S(2)}) collective-permute-start(bf16[4,15,3,8,128]{4,3,0,2,1:T(8,128)(2,1)S(1)} %constant_dynamic-update-slice_fusion.4), channel_id=1, source_target_pairs={{0,8},{1,9},{2,10},{3,11},{4,12},{5,13},{6,14},{7,15},{8,0},{9,1},... | collective-permute-start | bytes 1105928 | tf_op jit(solution)/shard_map/ppermute | solution.py:293
  33.3 1.5 %broadcast_in_dim.18 = bf16[16,15,3,8,128]{4,3,0,2,1:T(8,128)(2,1)} broadcast(bf16[]{:T(256)} %constant.74.clone.1), dimensions={} | broadcast | bytes 1474562 | tf_op jit(solution)/shard_map/broadcast_in_dim | solution.py:286
  34.8 0.0 copy-start.7
  34.8 0.0 copy-start.6
  34.8 0.0 copy-start.5
  34.8 0.8 constant_dynamic-update-slice_fusion.3
  35.6 0.0 collective-permute-done.3
  35.6 1.8 %constant_dynamic-update-slice_fusion.2 = bf16[16,15,3,8,128]{4,3,0,2,1:T(8,128)(2,1)} fusion(bf16[16,15,3,8,128]{4,3,0,2,1:T(8,128)(2,1)} %constant_dynamic-update-slice_fusion.3, bf16[4,15,3,8,128]{4,3,0,2,1:T(8,128)(2,1)} %collective-permute-done.3, s32[]{:T(128)S(6)} %select_n.50), kind=kLoop, calls=%fused_computation.12 | loop fusion | bytes 737284 | tf_op jit(solution)/shard_map/dynamic_update_slice | solution.py:295
  37.4 0.0 copy-start
  37.4 0.0 copy-start.1
  37.4 0.0 copy-start.2
  37.4 0.0 copy-start.4
  37.4 0.0 collective-permute-done.4
  37.4 0.8 constant_dynamic-update-slice_fusion.1
  38.2 25.4 %collective-permute-done.5 = bf16[4,15,3,8,128]{4,3,0,2,1:T(8,128)(2,1)S(1)} collective-permute-done((bf16[4,15,3,8,128]{4,3,0,2,1:T(8,128)(2,1)S(1)}, bf16[4,15,3,8,128]{4,3,0,2,1:T(8,128)(2,1)S(1)}, u32[]{:S(2)}, u32[]{:S(2)}) %collective-permute-start.5) | collective-permute-done | bytes 368672 | tf_op jit(solution)/shard_map/ppermute | solution.py:293
  63.6 0.8 constant_dynamic-update-slice_fusion
  64.4 1.0 collective-permute-start.6
  65.4 0.0 copy-done.7
  65.4 0.0 copy-done.6
  65.4 0.0 copy-done.5
  65.5 3.1 %collective-permute-done.6 = bf16[16,15,3,8,128]{4,3,0,2,1:T(8,128)(2,1)} collective-permute-done((bf16[16,15,3,8,128]{4,3,0,2,1:T(8,128)(2,1)}, bf16[16,15,3,8,128]{4,3,0,2,1:T(8,128)(2,1)}, u32[]{:S(2)}, u32[]{:S(2)}) %collective-permute-start.6) | collective-permute-done | bytes 1474592 | tf_op jit(solution)/shard_map/ppermute | solution.py:328
  68.6 0.0 all-to-all-done
  68.6 0.0 copy-done
  68.7 0.0 copy-done.1
  68.7 0.0 copy-done.2
  68.7 0.0 copy-done.4
  68.7 14.5 %shard_map.132 = bf16[2048,512]{1,0:T(8,128)(2,1)S(1)} custom-call(bf16[2048,512]{1,0:T(8,128)(2,1)S(1)} %bitcast.17, s32[2,2048]{1,0:T(2,128)S(1)} %copy-done, f32[1,2048]{1,0:T(1,128)S(1)} %bitcast.20, s32[2,1024]{1,0:T(2,128)S(1)} %copy-done.2, f32[1,1024]{1,0:T(1,128)S(1)} %bitcast.21, f32[32,1024]{1,0:T(8,128)S(1)} %pad.4.scale_ref, ...), custom_call_target="tpu_custom_call" | custom-call | flops 6039797760 | bytes 4194304 | tf_op jit(solution)/shard_map/pallas_call | solution.py:279
  83.2 0.0 copy-start.3
  83.2 37.2 %all_to_all.22 = bf16[128,16,512]{2,1,0:T(8,128)(2,1)S(1)} all-to-all(bf16[128,16,512]{2,1,0:T(8,128)(2,1)S(1)} %bitcast.18), channel_id=1, replica_groups=mesh['lat'=8,'lon'=16] {'lat','lon'}, dimensions={0} | all-to-all | bytes 4194304 | tf_op jit(solution)/shard_map/all_to_all | solution.py:302
  120.4 0.0 copy-done.3
  120.4 5.3 %shard_map.133 = (bf16[3,2048,128]{2,1,0:T(8,128)(2,1)}, bf16[2048,128]{1,0:T(8,128)(2,1)}) custom-call(s32[1,2048]{1,0:T(1,128)S(1)} %copy-done.3, bf16[2048,512]{1,0:T(8,128)(2,1)S(1)} %bitcast.19), custom_call_target="tpu_custom_call" | custom-call | flops 4294967296 | bytes 4194304 | tf_op jit(solution)/shard_map/pallas_call | solution.py:139
  (8 shorter events, 0.1 us)
Async XLA Ops:
  1.7 5.3 %collective-permute-start = (bf16[1,15,3,8,128]{4,3,0,2,1:T(8,128)(2,1)S(1)}, bf16[1,15,3,8,128]{4,3,0,2,1:T(8,128)(2,1)S(1)}, u32[]{:S(2)}, u32[]{:S(2)}) collective-permute-start(bf16[1,15,3,8,128]{4,3,0,2,1:T(8,128)(2,1)S(1)} %get-tuple-element.7), channel_id=1, source_target_pairs={{0,1},{1,2},{2,3},{3,0},{4,5},{5,6},{6,7},{7,4},{8,9},{9,10},{10,1... | collective-permute-start | bytes 276488 | tf_op jit(solution)/shard_map/ppermute | solution.py:293
  3.8 3.4 %collective-permute-start.1 = (bf16[1,15,3,8,128]{4,3,0,2,1:T(8,128)(2,1)S(1)}, bf16[1,15,3,8,128]{4,3,0,2,1:T(8,128)(2,1)S(1)}, u32[]{:S(2)}, u32[]{:S(2)}) collective-permute-start(bf16[1,15,3,8,128]{4,3,0,2,1:T(8,128)(2,1)S(1)} %get-tuple-element.7), channel_id=1, source_target_pairs={{0,3},{1,0},{2,1},{3,2},{4,7},{5,4},{6,5},{7,6},{8,11},{9,8},{10,9... | collective-permute-start | bytes 276488 | tf_op jit(solution)/shard_map/ppermute | solution.py:293
  5.1 5.2 %collective-permute-start.2 = (bf16[1,15,3,8,128]{4,3,0,2,1:T(8,128)(2,1)S(1)}, bf16[1,15,3,8,128]{4,3,0,2,1:T(8,128)(2,1)S(1)}, u32[]{:S(2)}, u32[]{:S(2)}) collective-permute-start(bf16[1,15,3,8,128]{4,3,0,2,1:T(8,128)(2,1)S(1)} %get-tuple-element.7), channel_id=1, source_target_pairs={{0,2},{1,3},{2,0},{3,1},{4,6},{5,7},{6,4},{7,5},{8,10},{9,11},{10,... | collective-permute-start | bytes 276488 | tf_op jit(solution)/shard_map/ppermute | solution.py:293
  10.3 25.3 %collective-permute-start.3 = (bf16[4,15,3,8,128]{4,3,0,2,1:T(8,128)(2,1)S(1)}, bf16[4,15,3,8,128]{4,3,0,2,1:T(8,128)(2,1)}, u32[]{:S(2)}, u32[]{:S(2)}) collective-permute-start(bf16[4,15,3,8,128]{4,3,0,2,1:T(8,128)(2,1)S(1)} %constant_dynamic-update-slice_fusion.4), channel_id=1, source_target_pairs={{0,4},{1,5},{2,6},{3,7},{4,8},{5,9},{6,10},{7,11},{8,12},{9,13},{1... | collective-permute-start | bytes 1105928 | tf_op jit(solution)/shard_map/ppermute | solution.py:293
  11.7 25.7 %collective-permute-start.4 = (bf16[4,15,3,8,128]{4,3,0,2,1:T(8,128)(2,1)S(1)}, bf16[4,15,3,8,128]{4,3,0,2,1:T(8,128)(2,1)S(1)}, u32[]{:S(2)}, u32[]{:S(2)}) collective-permute-start(bf16[4,15,3,8,128]{4,3,0,2,1:T(8,128)(2,1)S(1)} %constant_dynamic-update-slice_fusion.4), channel_id=1, source_target_pairs={{0,12},{1,13},{2,14},{3,15},{4,0},{5,1},{6,2},{7,3},{8,4},{9,5},{1... | collective-permute-start | bytes 1105928 | tf_op jit(solution)/shard_map/ppermute | solution.py:293
  20.1 48.5 %all-to-all-start = ((bf16[128,16,512]{2,1,0:T(8,128)(2,1)}), bf16[128,16,512]{2,1,0:T(8,128)(2,1)S(1)}, u32[]{:S(2)}, u32[]{:S(2)}) async-start(bf16[128,16,512]{2,1,0:T(8,128)(2,1)} %bitcast.22), calls=%async_computation | async-start | bytes 4194304 | tf_op jit(solution)/shard_map/all_to_all | solution.py:302
  30.4 33.2 %collective-permute-start.5 = (bf16[4,15,3,8,128]{4,3,0,2,1:T(8,128)(2,1)S(1)}, bf16[4,15,3,8,128]{4,3,0,2,1:T(8,128)(2,1)S(1)}, u32[]{:S(2)}, u32[]{:S(2)}) collective-permute-start(bf16[4,15,3,8,128]{4,3,0,2,1:T(8,128)(2,1)S(1)} %constant_dynamic-update-slice_fusion.4), channel_id=1, source_target_pairs={{0,8},{1,9},{2,10},{3,11},{4,12},{5,13},{6,14},{7,15},{8,0},{9,1},... | collective-permute-start | bytes 1105928 | tf_op jit(solution)/shard_map/ppermute | solution.py:293
  34.8 30.6 %copy-start.7 = (s32[1024]{0:T(1024)S(1)}, s32[1024]{0:T(1024)}, u32[]{:S(2)}) copy-start(s32[1024]{0:T(1024)} %param.21) | copy-start | bytes 12292
  34.8 30.6 %copy-start.6 = (f32[14,1024]{1,0:T(8,128)S(1)}, f32[14,1024]{1,0:T(8,128)}, u32[]{:S(2)}) copy-start(f32[14,1024]{1,0:T(8,128)} %param.20) | copy-start | bytes 172036
  34.8 30.6 %copy-start.5 = (f32[16,1024]{1,0:T(8,128)S(1)}, f32[16,1024]{1,0:T(8,128)}, u32[]{:S(2)}) copy-start(f32[16,1024]{1,0:T(8,128)} %param.19) | copy-start | bytes 196612
  37.4 31.3 %copy-start = (s32[2,2048]{1,0:T(2,128)S(1)}, s32[2,2048]{1,0:T(2,128)}, u32[]{:S(2)}) copy-start(s32[2,2048]{1,0:T(2,128)} %bidx_ref.1) | copy-start | bytes 49156
  37.4 31.3 %copy-start.1 = (f32[2048]{0:T(1024)S(1)}, f32[2048]{0:T(1024)}, u32[]{:S(2)}) copy-start(f32[2048]{0:T(1024)} %param.18) | copy-start | bytes 24580
  37.4 31.3 %copy-start.2 = (s32[2,1024]{1,0:T(2,128)S(1)}, s32[2,1024]{1,0:T(2,128)}, u32[]{:S(2)}) copy-start(s32[2,1024]{1,0:T(2,128)} %cidx_ref.1) | copy-start | bytes 24580
  37.4 31.3 %copy-start.4 = (f32[1024]{0:T(1024)S(1)}, f32[1024]{0:T(1024)}, u32[]{:S(2)}) copy-start(f32[1024]{0:T(1024)} %param.16) | copy-start | bytes 12292
  64.4 4.2 %collective-permute-start.6 = (bf16[16,15,3,8,128]{4,3,0,2,1:T(8,128)(2,1)}, bf16[16,15,3,8,128]{4,3,0,2,1:T(8,128)(2,1)}, u32[]{:S(2)}, u32[]{:S(2)}) collective-permute-start(bf16[16,15,3,8,128]{4,3,0,2,1:T(8,128)(2,1)} %constant_dynamic-update-slice_fusion), channel_id=1, source_target_pairs={{0,16},{16,0},{32,48},{48,32},{64,80},{80,64},{96,112},{112,96},{1... | collective-permute-start | bytes 4423688 | tf_op jit(solution)/shard_map/ppermute | solution.py:328
  83.2 37.2 %copy-start.3 = (s32[1,2048]{1,0:T(1,128)S(1)}, s32[1,2048]{1,0:T(1,128)}, u32[]{:S(2)}) copy-start(s32[1,2048]{1,0:T(1,128)} %perm_ref.1) | copy-start | bytes 24580

commit v2 on v1

--- a/solution.py
+++ b/solution.py
@@ -12,10 +12,12 @@
 MIB = 1 << 20
 
 
-def call(kernel, out, flops, limit, scratch=(), specs=None, out_specs=None):
+def call(kernel, out, flops, limit, scratch=(), specs=None, out_specs=None, aliases=None):
     extra = {} if specs is None else {"in_specs": specs}
     if out_specs is not None:
         extra["out_specs"] = out_specs
+    if aliases is not None:
+        extra["input_output_aliases"] = aliases
     return pl.pallas_call(
         kernel,
         out_shape=out,
@@ -33,13 +35,12 @@
     return [sum(blocks[:k]) for k in range(len(blocks))]
 
 
-def pick_kernel(perm_hbm, planes_hbm, last_hbm, out_hbm, perm_ref, data_ref, hot_ref, out_ref, in_sems, out_sems):
+def pick_kernel(perm_hbm, planes_hbm, out_hbm, perm_ref, data_ref, hot_ref, out_ref, in_sems, out_sems):
     total = perm_ref.shape[1]
     planes = planes_hbm.shape[0]
-    first = pltpu.make_async_copy(perm_hbm, perm_ref, in_sems.at[planes + 1])
+    first = pltpu.make_async_copy(perm_hbm, perm_ref, in_sems.at[planes])
     first.start()
     loads = [pltpu.make_async_copy(planes_hbm.at[v], data_ref.at[v], in_sems.at[v]) for v in range(planes)]
-    loads.append(pltpu.make_async_copy(last_hbm, data_ref.at[planes], in_sems.at[planes]))
     for load in loads:
         load.start()
     first.wait()
@@ -56,7 +57,7 @@
         load.wait()
     stores = []
     for k, (start, rows) in enumerate(zip(starts(PICK_BLOCKS), PICK_BLOCKS)):
-        data = jnp.concatenate([data_ref[v] for v in range(planes + 1)], axis=1)
+        data = jnp.concatenate([data_ref[v] for v in range(planes)], axis=1)
         got = jnp.dot(hot_ref[k % 2, :rows, :], data, preferred_element_type=F32)
         out_ref[start : start + rows, :] = got.astype(BF16)
         stores.append(
@@ -71,9 +72,9 @@
         store.wait()
 
 
-def pick(perm, planes, last):
+def pick(perm, planes):
     total = perm.shape[1]
-    count = planes.shape[0] + 1
+    count = planes.shape[0]
     out = jax.ShapeDtypeStruct((total, count * 128), BF16)
     far = pl.BlockSpec(memory_space=pl.ANY)
     scratch = [
@@ -85,7 +86,7 @@
         pltpu.SemaphoreType.DMA((len(PICK_BLOCKS),)),
     ]
     flops = 2 * total * total * count * 128
-    return call(pick_kernel, out, flops, 60, scratch, [far] * 3, far)(perm, planes, last)
+    return call(pick_kernel, out, flops, 60, scratch, [far] * 2, far)(perm, planes)
 
 
 RESTORE_BLOCKS = (1024, 512, 512)
@@ -160,8 +161,8 @@
     lax.fori_loop(0, rows // block, step, 0)
 
 
-def radiation_kernel(
-    data_ref,
+def adjoint_kernel(
+    cot_ref,
     bidx_ref,
     bw_ref,
     cidx_ref,
@@ -169,21 +170,21 @@
     scale_ref,
     ta_hbm,
     tb_hbm,
-    out_ref,
+    out_hbm,
+    back_hbm,
+    tt_hbm,
     ta_ref,
     tb_ref,
-    sems,
     back_ref,
     coarse_ref,
     tt_ref,
     rows_ref,
     adj_ref,
-    mid_ref,
-    heat_ref,
+    grad_ref,
+    sems,
 ):
     bands, width, _ = ta_ref.shape
     cols, rows = coarse_ref.shape
-
     loads = [
         pltpu.make_async_copy(ta_hbm, ta_ref, sems.at[0]),
         pltpu.make_async_copy(tb_hbm, tb_ref, sems.at[1]),
@@ -191,92 +192,152 @@
     for load in loads:
         load.start()
     two_hot(bidx_ref, bw_ref, back_ref)
+    store_back = pltpu.make_async_copy(back_ref, back_hbm, sems.at[2])
+    store_back.start()
     two_hot(cidx_ref, cw_ref, coarse_ref)
 
     def adjoint(i, carry):
         s = pl.multiple_of(i * 512, 512)
-        adj_ref[:, pl.ds(s, 512)] = jnp.dot(back_ref[pl.ds(s, 512), :], data_ref[:, width:], preferred_element_type=F32).T
-        return carry
-
-    def lift(i, carry):
-        s = pl.multiple_of(i * 1024, 1024)
-        tables = [ref[b] for ref in (ta_ref, tb_ref) for b in range(bands)]
-        adj = adj_ref[:, pl.ds(s, 1024)]
-        lifted = jnp.concatenate(
-            [(adj * scale_ref[b : b + 1, pl.ds(s, 1024)]).astype(BF16) for b in range(2 * bands)], axis=0
-        )
-        got = jnp.dot(jnp.concatenate(tables, axis=1), lifted, preferred_element_type=F32)
-        rows_ref[pl.ds(s, 1024), :] = got.T.astype(BF16)
-        return carry
-
-    def scatter(i, carry):
-        start = pl.multiple_of(i * 1024, 1024)
-        out_ref[pl.ds(start, 1024), :width] = jnp.dot(
-            coarse_ref[pl.ds(start, 1024), :], rows_ref[...], preferred_element_type=F32
-        ).astype(BF16)
-        return carry
-
-    def interpolate(i, carry):
-        s = pl.multiple_of(i * 1024, 1024)
-        mid_ref[:, pl.ds(s, 1024)] = lax.dot_general(
-            data_ref[:, :width], coarse_ref[:, pl.ds(s, 1024)], (((0,), (0,)), ((), ())), preferred_element_type=F32
-        ).astype(BF16)
-        return carry
-
-    def heat(i, carry):
-        s = pl.multiple_of(i * 1024, 1024)
-        mid = mid_ref[:, pl.ds(s, 1024)]
-        lifted = jnp.concatenate(
-            [
-                mid * jnp.broadcast_to(scale_ref[b : b + 1, pl.ds(s, 1024)].astype(BF16), mid.shape)
-                for b in range(2 * bands)
-            ],
-            axis=0,
-        )
-        heat_ref[:, pl.ds(s, 1024)] = jnp.dot(tt_ref[...], lifted, preferred_element_type=F32).astype(BF16)
-        return carry
-
-    def back(i, carry):
-        s = pl.multiple_of(i * 2048, 2048)
-        tendency = jnp.dot(heat_ref[...], back_ref[:, pl.ds(s, 2048)], preferred_element_type=F32)
-        out_ref[pl.ds(s, 2048), width:] = tendency.T.astype(BF16)
+        adj_ref[:, pl.ds(s, 512)] = jnp.dot(
+            back_ref[pl.ds(s, 512), :], cot_ref[...], preferred_element_type=F32
+        ).T
         return carry
 
     lax.fori_loop(0, rows // 512, adjoint, 0)
     for load in loads:
         load.wait()
-    lax.fori_loop(0, rows // 1024, lift, 0)
-    lax.fori_loop(0, cols // 1024, scatter, 0)
-    lax.fori_loop(0, rows // 1024, interpolate, 0)
     for part, ref in enumerate((ta_ref, tb_ref)):
         for b in range(bands):
             at = (part * bands + b) * width
             tt_ref[:, at : at + width] = ref[b].T
-    lax.fori_loop(0, rows // 1024, heat, 0)
-    lax.fori_loop(0, cols // 2048, back, 0)
-
-
-def radiation(data, bidx, bw, cidx, cw, scale, ta, tb):
+    store_turned = pltpu.make_async_copy(tt_ref, tt_hbm, sems.at[3])
+    store_turned.start()
+    tables = [ref[b] for ref in (ta_ref, tb_ref) for b in range(bands)]
+    lifted = jnp.concatenate(
+        [(adj_ref[...] * scale_ref[b : b + 1, :]).astype(BF16) for b in range(2 * bands)], axis=0
+    )
+    rows_ref[...] = jnp.dot(
+        jnp.concatenate(tables, axis=1), lifted, preferred_element_type=F32
+    ).astype(BF16)
+
+    def scatter(i, carry):
+        s = pl.multiple_of(i * 1024, 1024)
+        got = lax.dot_general(
+            rows_ref[...],
+            coarse_ref[pl.ds(s, 1024), :],
+            (((1,), (1,)), ((), ())),
+            preferred_element_type=F32,
+        )
+        grad_ref[pl.ds(s, 1024), :] = got.T.astype(BF16)
+        return carry
+
+    lax.fori_loop(0, cols // 1024, scatter, 0)
+    store_grad = pltpu.make_async_copy(grad_ref, out_hbm.at[:, pl.ds(0, width)], sems.at[4])
+    store_grad.start()
+    for store in (store_back, store_turned, store_grad):
+        store.wait()
+
+
+def adjoint_part(cot, bidx, bw, cidx, cw, scale, ta, tb):
     cols, rows = bw.shape[1], cw.shape[1]
     bands, width, levels = ta.shape
-    out = jax.ShapeDtypeStruct((cols, width + levels), BF16)
-    flops = 8 * bands * rows * levels * width
+    turned = (levels, 2 * bands * width)
+    out = [
+        jax.ShapeDtypeStruct((cols, width + levels), BF16),
+        jax.ShapeDtypeStruct((rows, cols), BF16),
+        jax.ShapeDtypeStruct(turned, BF16),
+    ]
     scratch = [
         pltpu.VMEM(ta.shape, BF16),
         pltpu.VMEM(tb.shape, BF16),
-        pltpu.SemaphoreType.DMA((2,)),
         pltpu.VMEM((rows, cols), BF16),
         pltpu.VMEM((cols, rows), BF16),
-        pltpu.VMEM((levels, 2 * bands * width), BF16),
-        pltpu.VMEM((rows, width), BF16),
+        pltpu.VMEM(turned, BF16),
+        pltpu.VMEM((width, rows), BF16),
         pltpu.VMEM((levels, rows), F32),
+        pltpu.VMEM((cols, width), BF16),
+        pltpu.SemaphoreType.DMA((5,)),
+    ]
+    near, far = pl.BlockSpec(memory_space=pltpu.VMEM), pl.BlockSpec(memory_space=pl.ANY)
+    flops = 4 * bands * rows * levels * width
+    kernel = call(adjoint_kernel, out, flops, 60, scratch, [near] * 6 + [far] * 2, [far] * 3)
+    return kernel(cot, bidx, bw, cidx, cw, scale, ta, tb)
+
+
+def forward_kernel(
+    fields_ref,
+    cidx_ref,
+    cw_ref,
+    scale_ref,
+    back_hbm,
+    tt_hbm,
+    whole_hbm,
+    out_hbm,
+    back_ref,
+    coarse_ref,
+    tt_ref,
+    mid_ref,
+    heat_ref,
+    tend_ref,
+    sems,
+):
+    del whole_hbm
+    width = fields_ref.shape[1]
+    rows = coarse_ref.shape[1]
+    bands = tt_ref.shape[1] // width
+    loads = [
+        pltpu.make_async_copy(tt_hbm, tt_ref, sems.at[0]),
+        pltpu.make_async_copy(back_hbm, back_ref, sems.at[1]),
+    ]
+    for load in loads:
+        load.start()
+    two_hot(cidx_ref, cw_ref, coarse_ref)
+
+    def interpolate(i, carry):
+        s = pl.multiple_of(i * 512, 512)
+        mid_ref[:, pl.ds(s, 512)] = lax.dot_general(
+            fields_ref[...],
+            coarse_ref[:, pl.ds(s, 512)],
+            (((0,), (0,)), ((), ())),
+            preferred_element_type=F32,
+        ).astype(BF16)
+        return carry
+
+    lax.fori_loop(0, rows // 512, interpolate, 0)
+    loads[0].wait()
+    lifted = jnp.concatenate(
+        [
+            mid_ref[...] * jnp.broadcast_to(scale_ref[b : b + 1, :].astype(BF16), mid_ref.shape)
+            for b in range(bands)
+        ],
+        axis=0,
+    )
+    heat_ref[...] = jnp.dot(tt_ref[...], lifted, preferred_element_type=F32).astype(BF16)
+    loads[1].wait()
+    tend_ref[...] = jnp.dot(heat_ref[...], back_ref[...], preferred_element_type=F32).T.astype(BF16)
+    store = pltpu.make_async_copy(tend_ref, out_hbm.at[:, pl.ds(width, tend_ref.shape[1])], sems.at[2])
+    store.start()
+    store.wait()
+
+
+def forward_part(fields, cidx, cw, scale, back, turned, whole):
+    cols, width = fields.shape
+    rows = cw.shape[1]
+    levels = turned.shape[0]
+    out = jax.ShapeDtypeStruct(whole.shape, BF16)
+    scratch = [
+        pltpu.VMEM(back.shape, BF16),
+        pltpu.VMEM((cols, rows), BF16),
+        pltpu.VMEM(turned.shape, BF16),
         pltpu.VMEM((width, rows), BF16),
         pltpu.VMEM((levels, rows), BF16),
+        pltpu.VMEM((cols, levels), BF16),
+        pltpu.SemaphoreType.DMA((3,)),
     ]
     near, far = pl.BlockSpec(memory_space=pltpu.VMEM), pl.BlockSpec(memory_space=pl.ANY)
-    specs = [near] * 6 + [far] * 2
-    kernel = call(radiation_kernel, out, flops, 34, scratch, specs)
-    return kernel(data, bidx, bw, cidx, cw, scale, ta, tb)
+    flops = 2 * turned.shape[1] * rows * levels
+    kernel = call(forward_kernel, out, flops, 60, scratch, [near] * 4 + [far] * 3, far, {6: 0})
+    return kernel(fields, cidx, cw, scale, back, turned, whole)
 
 
 def gather_four(block, stride):
@@ -335,10 +396,14 @@
 
     cw = coarse_weight[None]
     bw = back_weight[None]
-    planes = increments.transpose(1, 0, 2)
-    data = pick(owner_perm, planes, cotangent)
-    data = exchange(data, ALL)
-    back = radiation(data, back_index, bw, coarse_index, cw, scale, mine, other)
+    sent = pick(owner_perm, cotangent[None])
+    cot_rad = exchange(sent, ALL)
+    sent = pick(owner_perm, increments.transpose(1, 0, 2))
+    fields = exchange(sent, ALL)
+    whole, back_weights, turned = adjoint_part(
+        cot_rad, back_index, bw, coarse_index, cw, scale, mine, other
+    )
+    back = forward_part(fields, coarse_index, cw, scale, back_weights, turned, whole)
     back = exchange(back, ALL)
     gradient, tendency = restore(owner_perm, back)
     return (tendency, gradient.transpose(1, 0, 2))

time: 126 us -> 124 us (0.984)
  waiting for transfers between devices: 32 us -> 20.1 us
  Pallas kernels: 26.8 us -> 36.5 us
  starting transfers between devices: 22.1 us -> 25.7 us
  blocking collectives: 37.2 us -> 35 us
  local copies, waits for them, and re-layouts: 5.83 us -> 4.28 us
    ppermute x6, waiting for transfers between devices: 28.9 us -> 3.46 us  [gather_four(): got.append(lax.ppermute(block, 'lon', pairs))]
    all_to_all x1 -> x2, waiting for transfers between devices: 0.01 us -> 16.7 us  [exchange(): return lax.all_to_all(values, axes, split_axis=0, concat_axis=0, tiled=True)]
    pallas_call x2 -> x4, Pallas kernels: 21.4 us -> 31.2 us  [the longest x2 11 us: pick(): call(pick_kernel, out, flops, 60, scratch, [far] * 2, far)(perm, planes)]
    all_to_all x1 -> x2, starting transfers between devices: 10.2 us -> 15 us  [exchange(): return lax.all_to_all(values, axes, split_axis=0, concat_axis=0, tiled=True)]
    ppermute x1, waiting for transfers between devices: 3.14 us -> 0.01 us  [local(): other = lax.ppermute(whole, 'lat', partner)]
    dynamic_update_slice x7, local copies, waits for them, and re-layouts: 4.28 us -> 1.28 us  [gather_four(): lax.dynamic_update_slice_in_dim(out, piece, lax.rem(place + 4 - shift, 4)...]
    all_to_all x1, blocking collectives: 37.2 us -> 35 us  [exchange(): return lax.all_to_all(values, axes, split_axis=0, concat_axis=0, tiled=True)]
    unnamed x16 -> x14, local copies, waits for them, and re-layouts: 0.03 us -> 1.95 us
  transfers between devices with their start and end apart: 8 -> 9, of which waited for: 5 -> 5; matrix products, arithmetic and copies ran while one was open for 5% -> 2% of each run, Pallas kernels for 6% -> 18%
where the time goes in v2:
time: 124 us
  Pallas kernels  36.5 us (29%)
  blocking collectives  35 us (28%)
  starting transfers between devices  25.7 us (21%)
  waiting for transfers between devices  20.1 us (16%)
  local copies, waits for them, and re-layouts  4.28 us (3%)
    all_to_all x1, blocking collectives, exchange(): return lax.all_to_all(values, axes, split_axis=0, concat_axis=0, tiled=True)  35 us
    all_to_all x2, waiting for transfers between devices, exchange(): return lax.all_to_all(values, axes, split_axis=0, concat_axis=0, tiled=True)  16.7 us
    all_to_all x2, starting transfers between devices, exchange(): return lax.all_to_all(values, axes, split_axis=0, concat_axis=0, tiled=True)  15 us
    pallas_call x2, Pallas kernels, pick(): call(pick_kernel, out, flops, 60, scratch, [far] * 2, far)(perm, planes)  11 us
    pallas_call x1, Pallas kernels, adjoint_part(): return kernel(cot, bidx, bw, cidx, cw, scale, ta, tb)  11 us
    ppermute x6, starting transfers between devices, gather_four(): got.append(lax.ppermute(block, 'lon', pairs))  9.55 us
    pallas_call x1, Pallas kernels, forward_part(): return kernel(fields, cidx, cw, scale, back, turned, whole)  9.21 us
    pallas_call x1, Pallas kernels, restore(): call(restore_kernel, out, flops, 40, scratch, [near] * 2, [far] * 2)  5.32 us
  transfers between devices with their start and end apart: 9, of which 5 were waited for; matrix products, arithmetic and copies ran while one was open for 2% of the time, Pallas kernels for 18%

profile of v2, /device:TPU:1, one launch (start us, length us, event | category | flops | bytes accessed | tf_op | source)
XLA Modules:
  0.0 123.7 jit_solution(7398844305288385947)
XLA Ops:
  0.6 0.1 broadcast_in_dim.23
  0.7 1.0 constant_dynamic-update-slice_fusion.7
  1.7 2.1 %collective-permute-start = (bf16[1,15,3,8,128]{4,3,0,2,1:T(8,128)(2,1)S(1)}, bf16[1,15,3,8,128]{4,3,0,2,1:T(8,128)(2,1)S(1)}, u32[]{:S(2)}, u32[]{:S(2)}) collective-permute-start(bf16[1,15,3,8,128]{4,3,0,2,1:T(8,128)(2,1)S(1)} %get-tuple-element.13), channel_id=1, source_target_pairs={{0,1},{1,2},{2,3},{3,0},{4,5},{5,6},{6,7},{7,4},{8,9},{9,10},{10,1... | collective-permute-start | bytes 276488 | tf_op jit(solution)/shard_map/ppermute | solution.py:354
  3.8 1.4 %collective-permute-start.1 = (bf16[1,15,3,8,128]{4,3,0,2,1:T(8,128)(2,1)S(1)}, bf16[1,15,3,8,128]{4,3,0,2,1:T(8,128)(2,1)S(1)}, u32[]{:S(2)}, u32[]{:S(2)}) collective-permute-start(bf16[1,15,3,8,128]{4,3,0,2,1:T(8,128)(2,1)S(1)} %get-tuple-element.13), channel_id=1, source_target_pairs={{0,3},{1,0},{2,1},{3,2},{4,7},{5,4},{6,5},{7,6},{8,11},{9,8},{10,9... | collective-permute-start | bytes 276488 | tf_op jit(solution)/shard_map/ppermute | solution.py:354
  5.1 1.6 %collective-permute-start.2 = (bf16[1,15,3,8,128]{4,3,0,2,1:T(8,128)(2,1)S(1)}, bf16[1,15,3,8,128]{4,3,0,2,1:T(8,128)(2,1)S(1)}, u32[]{:S(2)}, u32[]{:S(2)}) collective-permute-start(bf16[1,15,3,8,128]{4,3,0,2,1:T(8,128)(2,1)S(1)} %get-tuple-element.13), channel_id=1, source_target_pairs={{0,2},{1,3},{2,0},{3,1},{4,6},{5,7},{6,4},{7,5},{8,10},{9,11},{10,... | collective-permute-start | bytes 276488 | tf_op jit(solution)/shard_map/ppermute | solution.py:354
  6.8 0.2 collective-permute-done
  7.0 0.2 collective-permute-done.1
  7.2 3.1 %collective-permute-done.2 = bf16[1,15,3,8,128]{4,3,0,2,1:T(8,128)(2,1)S(1)} collective-permute-done((bf16[1,15,3,8,128]{4,3,0,2,1:T(8,128)(2,1)S(1)}, bf16[1,15,3,8,128]{4,3,0,2,1:T(8,128)(2,1)S(1)}, u32[]{:S(2)}, u32[]{:S(2)}) %collective-permute-start.2) | collective-permute-done | bytes 92192 | tf_op jit(solution)/shard_map/ppermute | solution.py:354
  10.3 1.4 %collective-permute-start.3 = (bf16[4,15,3,8,128]{4,3,0,2,1:T(8,128)(2,1)S(1)}, bf16[4,15,3,8,128]{4,3,0,2,1:T(8,128)(2,1)}, u32[]{:S(2)}, u32[]{:S(2)}) collective-permute-start(bf16[4,15,3,8,128]{4,3,0,2,1:T(8,128)(2,1)S(1)} %constant_dynamic-update-slice_fusion.4), channel_id=1, source_target_pairs={{0,4},{1,5},{2,6},{3,7},{4,8},{5,9},{6,10},{7,11},{8,12},{9,13},{1... | collective-permute-start | bytes 1105928 | tf_op jit(solution)/shard_map/ppermute | solution.py:354
  11.7 1.5 %collective-permute-start.4 = (bf16[4,15,3,8,128]{4,3,0,2,1:T(8,128)(2,1)S(1)}, bf16[4,15,3,8,128]{4,3,0,2,1:T(8,128)(2,1)S(1)}, u32[]{:S(2)}, u32[]{:S(2)}) collective-permute-start(bf16[4,15,3,8,128]{4,3,0,2,1:T(8,128)(2,1)S(1)} %constant_dynamic-update-slice_fusion.4), channel_id=1, source_target_pairs={{0,12},{1,13},{2,14},{3,15},{4,0},{5,1},{6,2},{7,3},{8,4},{9,5},{1... | collective-permute-start | bytes 1105928 | tf_op jit(solution)/shard_map/ppermute | solution.py:354
  13.2 1.6 %collective-permute-start.5 = (bf16[4,15,3,8,128]{4,3,0,2,1:T(8,128)(2,1)S(1)}, bf16[4,15,3,8,128]{4,3,0,2,1:T(8,128)(2,1)S(1)}, u32[]{:S(2)}, u32[]{:S(2)}) collective-permute-start(bf16[4,15,3,8,128]{4,3,0,2,1:T(8,128)(2,1)S(1)} %constant_dynamic-update-slice_fusion.4), channel_id=1, source_target_pairs={{0,8},{1,9},{2,10},{3,11},{4,12},{5,13},{6,14},{7,15},{8,0},{9,1},... | collective-permute-start | bytes 1105928 | tf_op jit(solution)/shard_map/ppermute | solution.py:354
  14.8 4.3 %shard_map.132 = bf16[2048,128]{1,0:T(8,128)(2,1)} custom-call(s32[1,2048]{1,0:T(1,128)} %perm_ref.1, bf16[1,2048,128]{2,1,0:T(8,128)(2,1)} %bitcast.30), custom_call_target="tpu_custom_call" | custom-call | flops 1073741824 | bytes 4194304 | tf_op jit(solution)/shard_map/pallas_call | solution.py:89
  19.1 10.2 %all-to-all-start.1 = ((bf16[128,16,128]{2,1,0:T(8,128)(2,1)}), bf16[128,16,128]{2,1,0:T(8,128)(2,1)S(1)}, u32[]{:S(2)}, u32[]{:S(2)}) async-start(bf16[128,16,128]{2,1,0:T(8,128)(2,1)} %bitcast.26), calls=%async_computation.1 | async-start | bytes 1048576 | tf_op jit(solution)/shard_map/all_to_all | solution.py:363
  29.4 0.3 broadcast_in_dim.22
  29.7 0.1 constant_dynamic-update-slice_fusion.3
  29.8 0.0 collective-permute-done.3
  29.8 1.0 constant_dynamic-update-slice_fusion.2
  30.9 0.0 collective-permute-done.4
  30.9 0.1 constant_dynamic-update-slice_fusion.1
  30.9 0.0 collective-permute-done.5
  30.9 0.1 constant_dynamic-update-slice_fusion
  31.0 0.0 copy-start.2
  31.0 1.1 collective-permute-start.6
  32.2 6.7 %shard_map.131 = bf16[2048,384]{1,0:T(8,128)(2,1)} custom-call(s32[1,2048]{1,0:T(1,128)} %perm_ref.1, bf16[3,2048,128]{2,1,0:T(8,128)(2,1)} %bitcast.29), custom_call_target="tpu_custom_call" | custom-call | flops 3221225472 | bytes 4194304 | tf_op jit(solution)/shard_map/pallas_call | solution.py:89
  38.8 0.0 copy-done.2
  38.9 4.4 %all-to-all-done.1 = bf16[128,16,128]{2,1,0:T(8,128)(2,1)S(1)} async-done(((bf16[128,16,128]{2,1,0:T(8,128)(2,1)}), bf16[128,16,128]{2,1,0:T(8,128)(2,1)S(1)}, u32[]{:S(2)}, u32[]{:S(2)}) %all-to-all-start.1) | async-done | bytes 524320 | tf_op jit(solution)/shard_map/all_to_all | solution.py:363
  43.2 0.0 copy-start.4
  43.2 0.0 copy-start.6
  43.2 0.0 copy-start.5
  43.2 0.0 copy-start.3
  43.2 0.8 copy-done.4
  44.0 4.8 %all-to-all-start = ((bf16[128,16,384]{2,1,0:T(8,128)(2,1)}), bf16[128,16,384]{2,1,0:T(8,128)(2,1)S(1)}, u32[]{:S(2)}, u32[]{:S(2)}) async-start(bf16[128,16,384]{2,1,0:T(8,128)(2,1)} %bitcast.23), calls=%async_computation | async-start | bytes 3145728 | tf_op jit(solution)/shard_map/all_to_all | solution.py:363
  48.8 0.0 copy-done.6
  48.8 0.0 copy-done.5
  48.9 0.0 copy-done.3
  48.9 0.7 pad.4.scale_ref
  49.6 0.0 collective-permute-done.6
  49.6 11.0 %shard_map.133 = (bf16[2048,512]{1,0:T(8,128)(2,1)}, bf16[1024,2048]{1,0:T(8,128)(2,1)}, bf16[128,11520]{1,0:T(8,128)(2,1)}) custom-call(bf16[2048,128]{1,0:T(8,128)(2,1)} %bitcast.25, s32[2,2048]{1,0:T(2,128)} %bidx_ref.1, f32[1,2048]{1,0:T(1,128)} %bitcast.31, s32[2,1024]{1,0:T(2,128)} %cidx_ref.3, f32[1,1024]{1,0:T(1,128)} %bitcast.27, ...), custom_call_target="tpu_custom_call" | custom-call | flops 3019898880 | bytes 4194304 | tf_op jit(solution)/shard_map/pallas_call | solution.py:264
  60.6 12.3 %all-to-all-done = bf16[128,16,384]{2,1,0:T(8,128)(2,1)S(1)} async-done(((bf16[128,16,384]{2,1,0:T(8,128)(2,1)}), bf16[128,16,384]{2,1,0:T(8,128)(2,1)S(1)}, u32[]{:S(2)}, u32[]{:S(2)}) %all-to-all-start) | async-done | bytes 1572896 | tf_op jit(solution)/shard_map/all_to_all | solution.py:363
  72.9 0.0 copy-start.1
  72.9 1.1 copy-done.1
  74.0 9.2 %shard_map.134 = bf16[2048,512]{1,0:T(8,128)(2,1)} custom-call(bf16[2048,384]{1,0:T(8,128)(2,1)} %bitcast.22, s32[2,1024]{1,0:T(2,128)} %cidx_ref.3, f32[1,1024]{1,0:T(1,128)} %bitcast.28, f32[32,1024]{1,0:T(8,128)} %pad.4.scale_ref, bf16[1024,2048]{1,0:T(8,128)(2,1)} %get-tuple-element.7.back_hbm, ...), custom_call_target="tpu_custom_call", output_to_operand_aliasing={{}: (6, {})} | custom-call | flops 3019898880 | bytes 4194304 | tf_op jit(solution)/shard_map/pallas_call | solution.py:340
  83.2 0.0 copy-start
  83.3 35.0 %all_to_all.33 = bf16[128,16,512]{2,1,0:T(8,128)(2,1)S(1)} all-to-all(bf16[128,16,512]{2,1,0:T(8,128)(2,1)} %bitcast.21), channel_id=1, replica_groups=mesh['lat'=8,'lon'=16] {'lat','lon'}, dimensions={0} | all-to-all | bytes 4194304 | tf_op jit(solution)/shard_map/all_to_all | solution.py:363
  118.2 0.0 copy-done
  118.2 5.3 %shard_map.135 = (bf16[3,2048,128]{2,1,0:T(8,128)(2,1)}, bf16[2048,128]{1,0:T(8,128)(2,1)}) custom-call(s32[1,2048]{1,0:T(1,128)S(1)} %copy-done, bf16[2048,512]{1,0:T(8,128)(2,1)S(1)} %bitcast.20), custom_call_target="tpu_custom_call" | custom-call | flops 4294967296 | bytes 4194304 | tf_op jit(solution)/shard_map/pallas_call | solution.py:140
  (7 shorter events, 0.1 us)
Async XLA Ops:
  1.7 5.3 %collective-permute-start = (bf16[1,15,3,8,128]{4,3,0,2,1:T(8,128)(2,1)S(1)}, bf16[1,15,3,8,128]{4,3,0,2,1:T(8,128)(2,1)S(1)}, u32[]{:S(2)}, u32[]{:S(2)}) collective-permute-start(bf16[1,15,3,8,128]{4,3,0,2,1:T(8,128)(2,1)S(1)} %get-tuple-element.13), channel_id=1, source_target_pairs={{0,1},{1,2},{2,3},{3,0},{4,5},{5,6},{6,7},{7,4},{8,9},{9,10},{10,1... | collective-permute-start | bytes 276488 | tf_op jit(solution)/shard_map/ppermute | solution.py:354
  3.8 3.4 %collective-permute-start.1 = (bf16[1,15,3,8,128]{4,3,0,2,1:T(8,128)(2,1)S(1)}, bf16[1,15,3,8,128]{4,3,0,2,1:T(8,128)(2,1)S(1)}, u32[]{:S(2)}, u32[]{:S(2)}) collective-permute-start(bf16[1,15,3,8,128]{4,3,0,2,1:T(8,128)(2,1)S(1)} %get-tuple-element.13), channel_id=1, source_target_pairs={{0,3},{1,0},{2,1},{3,2},{4,7},{5,4},{6,5},{7,6},{8,11},{9,8},{10,9... | collective-permute-start | bytes 276488 | tf_op jit(solution)/shard_map/ppermute | solution.py:354
  5.1 5.2 %collective-permute-start.2 = (bf16[1,15,3,8,128]{4,3,0,2,1:T(8,128)(2,1)S(1)}, bf16[1,15,3,8,128]{4,3,0,2,1:T(8,128)(2,1)S(1)}, u32[]{:S(2)}, u32[]{:S(2)}) collective-permute-start(bf16[1,15,3,8,128]{4,3,0,2,1:T(8,128)(2,1)S(1)} %get-tuple-element.13), channel_id=1, source_target_pairs={{0,2},{1,3},{2,0},{3,1},{4,6},{5,7},{6,4},{7,5},{8,10},{9,11},{10,... | collective-permute-start | bytes 276488 | tf_op jit(solution)/shard_map/ppermute | solution.py:354
  10.3 19.5 %collective-permute-start.3 = (bf16[4,15,3,8,128]{4,3,0,2,1:T(8,128)(2,1)S(1)}, bf16[4,15,3,8,128]{4,3,0,2,1:T(8,128)(2,1)}, u32[]{:S(2)}, u32[]{:S(2)}) collective-permute-start(bf16[4,15,3,8,128]{4,3,0,2,1:T(8,128)(2,1)S(1)} %constant_dynamic-update-slice_fusion.4), channel_id=1, source_target_pairs={{0,4},{1,5},{2,6},{3,7},{4,8},{5,9},{6,10},{7,11},{8,12},{9,13},{1... | collective-permute-start | bytes 1105928 | tf_op jit(solution)/shard_map/ppermute | solution.py:354
  11.7 19.2 %collective-permute-start.4 = (bf16[4,15,3,8,128]{4,3,0,2,1:T(8,128)(2,1)S(1)}, bf16[4,15,3,8,128]{4,3,0,2,1:T(8,128)(2,1)S(1)}, u32[]{:S(2)}, u32[]{:S(2)}) collective-permute-start(bf16[4,15,3,8,128]{4,3,0,2,1:T(8,128)(2,1)S(1)} %constant_dynamic-update-slice_fusion.4), channel_id=1, source_target_pairs={{0,12},{1,13},{2,14},{3,15},{4,0},{5,1},{6,2},{7,3},{8,4},{9,5},{1... | collective-permute-start | bytes 1105928 | tf_op jit(solution)/shard_map/ppermute | solution.py:354
  13.2 17.7 %collective-permute-start.5 = (bf16[4,15,3,8,128]{4,3,0,2,1:T(8,128)(2,1)S(1)}, bf16[4,15,3,8,128]{4,3,0,2,1:T(8,128)(2,1)S(1)}, u32[]{:S(2)}, u32[]{:S(2)}) collective-permute-start(bf16[4,15,3,8,128]{4,3,0,2,1:T(8,128)(2,1)S(1)} %constant_dynamic-update-slice_fusion.4), channel_id=1, source_target_pairs={{0,8},{1,9},{2,10},{3,11},{4,12},{5,13},{6,14},{7,15},{8,0},{9,1},... | collective-permute-start | bytes 1105928 | tf_op jit(solution)/shard_map/ppermute | solution.py:354
  19.1 24.1 %all-to-all-start.1 = ((bf16[128,16,128]{2,1,0:T(8,128)(2,1)}), bf16[128,16,128]{2,1,0:T(8,128)(2,1)S(1)}, u32[]{:S(2)}, u32[]{:S(2)}) async-start(bf16[128,16,128]{2,1,0:T(8,128)(2,1)} %bitcast.26), calls=%async_computation.1 | async-start | bytes 1048576 | tf_op jit(solution)/shard_map/all_to_all | solution.py:363
  31.0 7.8 %copy-start.2 = (bf16[16,15,3,8,128]{4,3,0,2,1:T(8,128)(2,1)}, bf16[16,15,3,8,128]{4,3,0,2,1:T(8,128)(2,1)S(1)}, u32[]{:S(2)}) copy-start(bf16[16,15,3,8,128]{4,3,0,2,1:T(8,128)(2,1)S(1)} %constant_dynamic-update-slice_fusion) | copy-start | bytes 4423684
  31.0 18.6 %collective-permute-start.6 = (bf16[16,15,3,8,128]{4,3,0,2,1:T(8,128)(2,1)S(1)}, bf16[16,15,3,8,128]{4,3,0,2,1:T(8,128)(2,1)}, u32[]{:S(2)}, u32[]{:S(2)}) collective-permute-start(bf16[16,15,3,8,128]{4,3,0,2,1:T(8,128)(2,1)S(1)} %constant_dynamic-update-slice_fusion), channel_id=1, source_target_pairs={{0,16},{16,0},{32,48},{48,32},{64,80},{80,64},{96,112},{112,96},{1... | collective-permute-start | bytes 4423688 | tf_op jit(solution)/shard_map/ppermute | solution.py:389
  43.2 0.8 copy-start.4
  43.2 5.6 %copy-start.6 = (s32[1024]{0:T(1024)S(1)}, s32[1024]{0:T(1024)}, u32[]{:S(2)}) copy-start(s32[1024]{0:T(1024)} %param.21) | copy-start | bytes 12292
  43.2 5.6 %copy-start.5 = (f32[14,1024]{1,0:T(8,128)S(1)}, f32[14,1024]{1,0:T(8,128)}, u32[]{:S(2)}) copy-start(f32[14,1024]{1,0:T(8,128)} %param.20) | copy-start | bytes 172036
  43.2 5.6 %copy-start.3 = (f32[16,1024]{1,0:T(8,128)S(1)}, f32[16,1024]{1,0:T(8,128)}, u32[]{:S(2)}) copy-start(f32[16,1024]{1,0:T(8,128)} %param.19) | copy-start | bytes 196612
  44.0 28.9 %all-to-all-start = ((bf16[128,16,384]{2,1,0:T(8,128)(2,1)}), bf16[128,16,384]{2,1,0:T(8,128)(2,1)S(1)}, u32[]{:S(2)}, u32[]{:S(2)}) async-start(bf16[128,16,384]{2,1,0:T(8,128)(2,1)} %bitcast.23), calls=%async_computation | async-start | bytes 3145728 | tf_op jit(solution)/shard_map/all_to_all | solution.py:363
  72.9 1.1 copy-start.1
  83.2 35.0 %copy-start = (s32[1,2048]{1,0:T(1,128)S(1)}, s32[1,2048]{1,0:T(1,128)}, u32[]{:S(2)}) copy-start(s32[1,2048]{1,0:T(1,128)} %perm_ref.1) | copy-start | bytes 24580
